TPU v7x, 32 devices: a whole 2x2x4 slice. The times are simulated.
32 devices in a mesh: row: 4 (over y, core), col: 8 (over z, x).
Axes of the slice: x: 2, y: 2, z: 4, core: 2. Of those that a mesh axis runs over, the one named last changes fastest.
Arguments:
- acts: bfloat16 [192, 2, 28672], P('col', None, 'row'), may hold values from -6 to 6
- grads: bfloat16 [192, 2, 8192], P('row', None, 'col'), may hold values from -0.3984375 to 0.3984375
- basis_in: bfloat16 [28672, 28672], P('row', 'col'), may hold values from -0.03125 to 0.03125
- basis_out: bfloat16 [8192, 8192], P('col', 'row'), may hold values from -0.0625 to 0.0625
- eigen: bfloat16 [28672, 8192], P('col', 'row'), may hold values from 0.5 to 8
- sketch: bfloat16 [72, 8192], P(None, 'col'), may hold values from -0.0625 to 0.0625
Outputs:
- range_basis: float32 [2, 72, 28672], P(None, None, 'row')
- projected: float32 [2, 72, 8192], P(None, None, 'col')
All inputs are finite; a program needn't handle non-finite values.
Results may differ from a plain program's by a relative error of at most 0.018.
Values may be sent and summed in bfloat16 or wider, within the bound.
A program may use at most 192 MiB of HBM per device.

v0:
```python
import functools
import jax
import jax.numpy as jnp
from jax import lax
from jax.experimental import pallas as pl
from jax.experimental.pallas import tpu as pltpu
from jax.sharding import PartitionSpec as P

MESH = pl.DeviceIdType.MESH
VMEM = pl.BlockSpec(memory_space=pltpu.VMEM)
BAND = 16


def greet(axis, n, me):
    barrier = pltpu.get_barrier_semaphore()
    for k in range(1, n):
        pl.semaphore_signal(
            barrier, inc=1, device_id={axis: lax.rem(me + k, n)}, device_id_type=MESH
        )
    pl.semaphore_wait(barrier, n - 1)


def send(src, dst, sems, k, axis, peer):
    copy = pltpu.make_async_remote_copy(
        src_ref=src,
        dst_ref=dst,
        send_sem=sems[0].at[k - 1],
        recv_sem=sems[1].at[k - 1],
        device_id={axis: peer},
        device_id_type=MESH,
    )
    copy.start()
    return copy


def columns(ref, index, width):
    return ref.at[:, pl.ds(pl.multiple_of(index * width, width), width)]


def gather_kernel(axis, n, leading, x_ref, o_ref, send_sem, recv_sem, own_sem):
    me = lax.axis_index(axis)
    place = o_ref.at[me] if leading else columns(o_ref, me, x_ref.shape[1])
    greet(axis, n, me)
    copies = [
        send(x_ref, place, (send_sem, recv_sem), k, axis, lax.rem(me + k, n)) for k in range(1, n)
    ]
    own = pltpu.make_async_copy(x_ref, place, own_sem)
    own.start()
    own.wait()
    for copy in copies:
        copy.wait()


def add_slots(slots, n, out):
    def step(i, carry):
        rows = pl.ds(pl.multiple_of(i * BAND, BAND), BAND)
        total = slots[0, rows, :].astype(jnp.float32)
        for k in range(1, n):
            total = total + slots[k, rows, :].astype(jnp.float32)
        out[rows, :] = total.astype(out.dtype)
        return carry

    lax.fori_loop(0, slots.shape[1] // BAND, step, 0)


def fill_slots(axis, n, me, x_ref, slots, sems, own_sem):
    width = slots.shape[2]
    greet(axis, n, me)
    copies = []
    for k in range(1, n):
        peer = lax.rem(me + k, n)
        copies.append(send(columns(x_ref, peer, width), slots.at[k], sems, k, axis, peer))
    own = pltpu.make_async_copy(columns(x_ref, me, width), slots.at[0], own_sem)
    own.start()
    own.wait()
    for copy in copies:
        copy.wait()


def scatter_kernel(axis, n, x_ref, o_ref, slots, send_sem, recv_sem, own_sem):
    me = lax.axis_index(axis)
    fill_slots(axis, n, me, x_ref, slots, (send_sem, recv_sem), own_sem)
    add_slots(slots, n, o_ref)


def reduce_kernel(
    axis, n, x_ref, o_ref, slots, stage, send_sem, recv_sem, own_sem, send_two, recv_two, own_two
):
    me = lax.axis_index(axis)
    fill_slots(axis, n, me, x_ref, slots, (send_sem, recv_sem), own_sem)
    add_slots(slots, n, stage)
    place = columns(o_ref, me, slots.shape[2])
    copies = [
        send(stage, place, (send_two, recv_two), k, axis, lax.rem(me + k, n)) for k in range(1, n)
    ]
    own = pltpu.make_async_copy(stage, place, own_two)
    own.start()
    own.wait()
    for copy in copies:
        copy.wait()


def semaphores(n):
    return [
        pltpu.SemaphoreType.DMA((n - 1,)),
        pltpu.SemaphoreType.DMA((n - 1,)),
        pltpu.SemaphoreType.DMA,
    ]


def launch(kernel, name, number, shape, dtype, scratch, x):
    return pl.pallas_call(
        kernel,
        name=name,
        out_shape=jax.ShapeDtypeStruct(shape, dtype),
        in_specs=[VMEM],
        out_specs=VMEM,
        scratch_shapes=scratch,
        compiler_params=pltpu.CompilerParams(
            collective_id=number, has_side_effects=True, vmem_limit_bytes=40 * 2**20
        ),
    )(x)


def fits(x, width):
    return x.shape[0] % BAND == 0 and width % 128 == 0


def gather_rows(x, axis, n, number):
    if not fits(x, x.shape[1]):
        return lax.all_gather(x, axis, axis=0, tiled=True)
    kernel = functools.partial(gather_kernel, axis, n, True)
    full = launch(kernel, f"gather{number}", number, (n, *x.shape), x.dtype, semaphores(n), x)
    return full.reshape(n * x.shape[0], x.shape[1])


def gather_columns(x, axis, n, number):
    if not fits(x, x.shape[1]):
        return lax.all_gather(x, axis, axis=1, tiled=True)
    kernel = functools.partial(gather_kernel, axis, n, False)
    shape = (x.shape[0], n * x.shape[1])
    return launch(kernel, f"gather{number}", number, shape, x.dtype, semaphores(n), x)


def scatter_sum(x, axis, n, number):
    width = x.shape[1] // n
    if not fits(x, width):
        return lax.psum_scatter(x.astype(jnp.float32), axis, scatter_dimension=1, tiled=True)
    scratch = [pltpu.VMEM((n, x.shape[0], width), x.dtype), *semaphores(n)]
    kernel = functools.partial(scatter_kernel, axis, n)
    shape = (x.shape[0], width)
    return launch(kernel, f"scatter{number}", number, shape, jnp.float32, scratch, x)


def full_sum(x, axis, n, number):
    width = x.shape[1] // n
    if not fits(x, width):
        return lax.psum(x.astype(jnp.float32), axis).astype(jnp.bfloat16)
    scratch = [
        pltpu.VMEM((n, x.shape[0], width), x.dtype),
        pltpu.VMEM((x.shape[0], width), jnp.bfloat16),
        *semaphores(n),
        *semaphores(n),
    ]
    kernel = functools.partial(reduce_kernel, axis, n)
    return launch(kernel, f"sum{number}", number, x.shape, jnp.bfloat16, scratch, x)


def dot(a, b, contract):
    product = lax.dot_general(a, b, ((contract), ((), ())), preferred_element_type=jnp.float32)
    return product


def on_device(nrow, ncol, acts, grads, basis_in, basis_out, eigen, sketch):
    bf = jnp.bfloat16
    queries = acts.shape[1]
    flat = queries * sketch.shape[0]
    full_acts = gather_rows(acts.reshape(-1, acts.shape[2]), "col", ncol, 0)
    tokens = full_acts.shape[0] // queries
    act_rot = full_sum(dot(full_acts, basis_in, ((1,), (0,))).astype(bf), "row", nrow, 1)
    full_grads = gather_rows(grads.reshape(-1, grads.shape[2]), "row", nrow, 2)
    joined = jnp.concatenate([full_grads, sketch], axis=0)
    joined = jnp.pad(joined, ((0, -joined.shape[0] % BAND), (0, 0)))
    joined_sum = full_sum(dot(joined, basis_out, ((1,), (0,))).astype(bf), "col", ncol, 3)
    grad_rot = joined_sum[: tokens * queries].reshape(tokens, queries, -1)
    sketch_rot = joined_sum[tokens * queries : tokens * queries + sketch.shape[0]]
    core_sum = jnp.einsum(
        "tqj,tqp->qjp",
        act_rot.reshape(tokens, queries, -1),
        grad_rot,
        preferred_element_type=jnp.float32,
    )
    scaled = (core_sum / eigen.astype(jnp.float32)).astype(bf)
    reduced_part = jnp.einsum("qjp,sp->qsj", scaled, sketch_rot, preferred_element_type=jnp.float32)
    reduced = full_sum(reduced_part.astype(bf).reshape(flat, -1), "row", nrow, 4)
    range_part = dot(reduced, basis_in, ((1,), (1,))).astype(bf)
    range_rows = scatter_sum(range_part, "col", ncol, 5).reshape(queries, sketch.shape[0], -1)
    gram_piece = jnp.einsum("qsi,qri->qsr", range_rows, range_rows, precision=lax.Precision.HIGHEST)
    gram = lax.psum(gram_piece, ("row", "col"))
    factor = jnp.linalg.cholesky(gram)
    basis_piece = lax.linalg.triangular_solve(factor, range_rows, left_side=True, lower=True)
    basis_rows = gather_columns(basis_piece.astype(bf).reshape(flat, -1), "col", ncol, 6)
    mapped_part = dot(basis_rows, basis_in, ((1,), (0,))).astype(bf)
    mapped = full_sum(mapped_part, "row", nrow, 7).reshape(queries, sketch.shape[0], -1)
    core_part = jnp.einsum("qsj,qjp->qsp", mapped, scaled, preferred_element_type=jnp.float32)
    core = full_sum(core_part.astype(bf).reshape(flat, -1), "col", ncol, 8)
    projection_part = dot(core, basis_out, ((1,), (1,))).astype(bf)
    projected = full_sum(projection_part, "row", nrow, 9)
    shape = (queries, sketch.shape[0], -1)
    return (
        basis_rows.astype(jnp.float32).reshape(shape),
        projected.astype(jnp.float32).reshape(shape),
    )


def solution(mesh):
    in_specs = (
        P("col", None, "row"),
        P("row", None, "col"),
        P("row", "col"),
        P("col", "row"),
        P("col", "row"),
        P(None, "col"),
    )
    out_specs = (P(None, None, "row"), P(None, None, "col"))
    body = functools.partial(on_device, mesh.shape["row"], mesh.shape["col"])
    return jax.shard_map(body, mesh=mesh, in_specs=in_specs, out_specs=out_specs, check_vma=False)
```

profile of v0, /device:TPU:0, one launch (start us, length us, event | category | flops | bytes accessed | tf_op | source)
XLA Modules:
  0.0 694.4 jit_solution(4478717053639674216)
XLA Ops:
  1.6 12.1 %gather2.1 = bf16[4,96,1024]{2,1,0:T(8,128)(2,1)S(1)} custom-call(bf16[96,1024]{1,0:T(8,128)(2,1)S(1)} %reshape.60.x_ref), custom_call_target="tpu_custom_call" | custom-call | tf_op jit(solution)/shard_map/gather2/pallas_call | solution.py:112
  13.7 4.4 convolution_convert_fusion.4.x_ref
  18.1 83.9 %sum3.1 = bf16[464,2048]{1,0:T(8,128)(2,1)S(1)} custom-call(bf16[464,2048]{1,0:T(8,128)(2,1)S(1)} %convolution_convert_fusion.4.x_ref), custom_call_target="tpu_custom_call" | custom-call | tf_op jit(solution)/shard_map/sum3/pallas_call | solution.py:112
  103.4 2.3 reshape.65
  105.7 16.6 %convert_element_type.39 = f32[3584,2048]{1,0:T(8,128)} convert(bf16[3584,2048]{1,0:T(8,128)(2,1)} %param.10) | non-fusion elementwise | flops 7340032 | bytes 44040192 | tf_op jit(solution)/shard_map/convert_element_type | solution.py:193
  122.5 104.1 %gather0.1 = bf16[8,48,7168]{2,1,0:T(8,128)(2,1)S(1)} custom-call(bf16[48,7168]{1,0:T(8,128)(2,1)S(1)} %reshape.62.x_ref), custom_call_target="tpu_custom_call" | custom-call | tf_op jit(solution)/shard_map/gather0/pallas_call | solution.py:112
  226.6 25.5 %convolution_convert_fusion.1.x_ref = bf16[384,3584]{1,0:T(8,128)(2,1)S(1)} fusion(bf16[384,7168]{1,0:T(8,128)(2,1)S(1)} %bitcast.45, bf16[7168,3584]{1,0:T(8,128)(2,1)} %param.8), kind=kOutput, calls=%fused_computation.2 | convolution fusion | flops 19731382272 | bytes 59637760 | tf_op jit(solution)/shard_map/dot_general | solution.py:170
  252.2 61.3 %sum1.1 = bf16[384,3584]{1,0:T(8,128)(2,1)S(1)} custom-call(bf16[384,3584]{1,0:T(8,128)(2,1)S(1)} %convolution_convert_fusion.1.x_ref), custom_call_target="tpu_custom_call" | custom-call | tf_op jit(solution)/shard_map/sum1/pallas_call | solution.py:112
  313.5 2.5 reshape.64
  316.0 22.8 %divide_convert_fusion = bf16[2,3584,2048]{2,1,0:T(8,128)(2,1)} fusion(f32[3584,2048]{1,0:T(8,128)} %convert_element_type.39, bf16[192,2,3584]{2,1,0:T(2,128)(2,1)} %reshape.64, bf16[192,2,2048]{2,1,0:T(2,128)(2,1)} %reshape.65), kind=kOutput, calls=%fused_computation | convolution fusion | flops 5666504704 | bytes 63045632 | tf_op jit(solution)/shard_map/tqj,tqp->qjp/dot_general | solution.py:187
  338.7 14.3 %convolution_convert_fusion.3 = bf16[72,2,3584]{2,0,1:T(8,128)(2,1)S(1)} fusion(bf16[2,3584,2048]{2,1,0:T(8,128)(2,1)} %divide_convert_fusion, bf16[464,2048]{1,0:T(8,128)(2,1)} %copy-done), kind=kOutput, calls=%fused_computation.4 | convolution fusion | flops 2114445312 | bytes 30687232 | tf_op jit(solution)/shard_map/qjp,sp->qsj/dot_general | solution.py:194
  353.1 26.0 %sum4.1 = bf16[144,3584]{1,0:T(8,128)(2,1)S(1)} custom-call(bf16[144,3584]{1,0:T(8,128)(2,1)S(1)} %bitcast.42), custom_call_target="tpu_custom_call" | custom-call | tf_op jit(solution)/shard_map/sum4/pallas_call | solution.py:112
  380.0 22.5 %convolution_convert_fusion.x_ref = bf16[144,7168]{1,0:T(8,128)(2,1)S(1)} fusion(bf16[144,3584]{1,0:T(8,128)(2,1)} %copy-done.1, bf16[7168,3584]{1,0:T(8,128)(2,1)} %param.8), kind=kOutput, calls=%fused_computation.1 | convolution fusion | flops 7399784448 | bytes 54476800 | tf_op jit(solution)/shard_map/dot_general | solution.py:170
  402.5 67.2 %scatter5.1 = f32[144,896]{1,0:T(8,128)S(1)} custom-call(bf16[144,7168]{1,0:T(8,128)(2,1)S(1)} %convolution_convert_fusion.x_ref), custom_call_target="tpu_custom_call" | custom-call | tf_op jit(solution)/shard_map/scatter5/pallas_call | solution.py:112
  470.3 53.6 %psum.7 = f32[2,72,72]{1,2,0:T(8,128)S(1)} all-reduce(f32[2,72,72]{1,2,0:T(8,128)S(1)} %fusion.18), channel_id=1, replica_groups=mesh['row'=4,'col'=8] {'row','col'}, use_global_device_ids=true, to_apply=%region_0.1 | all-reduce | flops 10368 | bytes 82944 | tf_op jit(solution)/shard_map/psum | solution.py:199
  524.0 13.2 %custom-call.7 = f32[2,72,72]{2,1,0:T(8,128)S(1)} custom-call(f32[2,72,72]{2,1,0:T(8,128)S(1)} %fusion.14), custom_call_target="Cholesky" | custom-call | tf_op jit(solution)/shard_map/jit(cholesky)/cholesky | solution.py:200
  537.5 11.1 %custom-call.8 = f32[2,1,72,72]{2,3,1,0:T(8,128)S(1)} custom-call(f32[2,1,72,72]{3,2,1,0:T(8,128)S(1)} %select_bitcast_fusion), custom_call_target="InvertDiagBlocksLowerTriangular" | custom-call | tf_op jit(solution)/shard_map/triangular_solve | solution.py:201
  549.3 35.1 %gather6.1 = bf16[144,7168]{1,0:T(8,128)(2,1)S(1)} custom-call(bf16[144,896]{1,0:T(8,128)(2,1)S(1)} %bitcast.48), custom_call_target="tpu_custom_call" | custom-call | tf_op jit(solution)/shard_map/gather6/pallas_call | solution.py:112
  584.4 18.1 %convolution_convert_fusion.2.x_ref = bf16[144,3584]{1,0:T(8,128)(2,1)S(1)} fusion(bf16[144,7168]{1,0:T(8,128)(2,1)S(1)} %gather6.1, bf16[7168,3584]{1,0:T(8,128)(2,1)} %param.8), kind=kOutput, calls=%fused_computation.3 | convolution fusion | flops 7399268352 | bytes 54476800 | tf_op jit(solution)/shard_map/dot_general | solution.py:170
  602.5 25.8 %sum7.1 = bf16[144,3584]{1,0:T(8,128)(2,1)S(1)} custom-call(bf16[144,3584]{1,0:T(8,128)(2,1)S(1)} %convolution_convert_fusion.2.x_ref), custom_call_target="tpu_custom_call" | custom-call | tf_op jit(solution)/shard_map/sum7/pallas_call | solution.py:112
  628.3 12.3 %convolution_convert_fusion.5 = bf16[2,72,2048]{2,1,0:T(8,128)(2,1)S(1)} fusion(bf16[2,72,3584]{2,1,0:T(8,128)(2,1)S(1)} %bitcast.41, bf16[2,3584,2048]{2,1,0:T(8,128)(2,1)} %divide_convert_fusion), kind=kOutput, calls=%fused_computation.7 | convolution fusion | flops 2114224128 | bytes 30982144 | tf_op jit(solution)/shard_map/qsj,qjp->qsp/dot_general | solution.py:205
  640.6 39.4 %sum8.1 = bf16[144,2048]{1,0:T(8,128)(2,1)S(1)} custom-call(bf16[144,2048]{1,0:T(8,128)(2,1)S(1)} %bitcast.46), custom_call_target="tpu_custom_call" | custom-call | tf_op jit(solution)/shard_map/sum8/pallas_call | solution.py:112
  681.6 9.5 %sum9.1 = bf16[144,1024]{1,0:T(8,128)(2,1)S(1)} custom-call(bf16[144,1024]{1,0:T(8,128)(2,1)S(1)} %convolution_convert_fusion.6.x_ref), custom_call_target="tpu_custom_call" | custom-call | tf_op jit(solution)/shard_map/sum9/pallas_call | solution.py:112
  692.0 2.4 convert.2
  (22 shorter events, 7.7 us)
Async XLA Ops:
  102.0 1.3 copy-start
  105.7 16.6 %copy-start.3 = (bf16[24,2,7168]{2,1,0:T(2,128)(2,1)S(1)}, bf16[24,2,7168]{2,1,0:T(2,128)(2,1)}, u32[]{:S(2)}) copy-start(bf16[24,2,7168]{2,1,0:T(2,128)(2,1)} %param.6) | copy-start | bytes 2064388
  379.1 1.0 copy-start.1
  628.3 51.7 %copy-start.2 = (bf16[1024,2048]{1,0:T(8,128)(2,1)S(1)}, bf16[1024,2048]{1,0:T(8,128)(2,1)}, u32[]{:S(2)}) copy-start(bf16[1024,2048]{1,0:T(8,128)(2,1)} %param.9) | copy-start | bytes 12582916
where the time goes:
time: 698 us; the launch traced here: 694 us
  Pallas kernels  464 us (66%)
  matrix products  123 us (18%)
  blocking collectives  53.6 us (8%)
  other arithmetic  44.5 us (6%)
  local copies, waits for them, and re-layouts  8.48 us (1%)
    pallas_call x10, Pallas kernels, launch(): pl.pallas_call(kernel, name=name, out_shape=jax.ShapeDtypeStruct(shape, d...  464 us
    dot_general x5, matrix products, dot(): lax.dot_general(a, b, (contract, ((), ())), preferred_element_type=jnp.fl...  72 us
    psum x1, blocking collectives, on_device(): gram = lax.psum(gram_piece, ('row', 'col'))  53.6 us
    dot_general x1, matrix products, on_device(): jnp.einsum('tqj,tqp->qjp', act_rot.reshape(tokens, queries, -1), grad_rot...  22.8 us
    convert_element_type x1, other arithmetic, on_device(): scaled = (core_sum / eigen.astype(jnp.float32)).astype(bf)  16.6 us
    dot_general x1, matrix products, on_device(): jnp.einsum('qjp,sp->qsj', scaled, sketch_rot, preferred_element_type=jnp....  14.3 us

commit v1 on v0

v1 whole, which is shorter than its diff:
```python
import functools
import jax
import jax.numpy as jnp
from jax import lax
from jax.experimental import pallas as pl
from jax.experimental.pallas import tpu as pltpu
from jax.sharding import PartitionSpec as P

MESH = pl.DeviceIdType.MESH
VMEM = pl.BlockSpec(memory_space=pltpu.VMEM)
BAND = 16
PIECES = 3
BF = jnp.bfloat16
F32 = jnp.float32


def remote(src, dst, send_sem, recv_sem, axis, peer):
    return pltpu.make_async_remote_copy(
        src_ref=src,
        dst_ref=dst,
        send_sem=send_sem,
        recv_sem=recv_sem,
        device_id={axis: peer},
        device_id_type=MESH,
    )


def greet(axis, n, me):
    barrier = pltpu.get_barrier_semaphore()
    for k in range(1, n):
        pl.semaphore_signal(
            barrier, inc=1, device_id={axis: lax.rem(me + k, n)}, device_id_type=MESH
        )
    pl.semaphore_wait(barrier, n - 1)


def columns(ref, index, width):
    return ref.at[:, pl.ds(pl.multiple_of(index * width, width), width)]


def line_gather(n, me, own, view, sems):
    z_send, z_recv, x_send, x_recv = sems
    nz = n // 2
    z, x = me // 2, lax.rem(me, 2)
    other = me + 1 - 2 * x

    def along(step, origin, c, src):
        block = view(origin * 2 + x, c)
        way = (step + 1) // 2
        return remote(
            src, block, z_send.at[way, origin, c], z_recv.at[origin, c], "col", me + 2 * step
        )

    def across(origin, c, src):
        block = view(origin * 2 + x, c)
        return remote(src, block, x_send.at[origin, c], x_recv.at[origin, c], "col", other)

    def arrived(origin, c):
        block = view(origin * 2 + x, c)
        remote(block, block, z_send.at[0, origin, c], z_recv.at[origin, c], "col", other).wait_recv()
        return block

    for c in range(PIECES):

        @pl.when(z < nz - 1)
        def _():
            along(1, z, c, own(c)).start()

        @pl.when(z > 0)
        def _():
            along(-1, z, c, own(c)).start()

        across(z, c, own(c)).start()

    for d in range(1, nz):
        for c in range(PIECES):

            @pl.when(z >= d)
            def _():
                block = arrived(z - d, c)

                @pl.when(z < nz - 1)
                def _():
                    along(1, z - d, c, block).start()

                across(z - d, c, block).start()

            @pl.when(z + d < nz)
            def _():
                block = arrived(z + d, c)

                @pl.when(z > 0)
                def _():
                    along(-1, z + d, c, block).start()

                across(z + d, c, block).start()

    def finish():
        for o in range(nz):
            for c in range(PIECES):
                across(o, c, view(o * 2 + x, c)).wait_send()
                block = view(o * 2 + 1 - x, c)
                remote(block, block, x_send.at[o, c], x_recv.at[o, c], "col", other).wait_recv()

                @pl.when((z < nz - 1) & (z >= o))
                def _():
                    along(1, o, c, view(o * 2 + x, c)).wait_send()

                @pl.when((z > 0) & (z <= o))
                def _():
                    along(-1, o, c, view(o * 2 + x, c)).wait_send()

    return finish


def gather_sems(n):
    nz = n // 2
    return [
        pltpu.SemaphoreType.DMA((2, nz, PIECES)),
        pltpu.SemaphoreType.DMA((nz, PIECES)),
        pltpu.SemaphoreType.DMA((nz, PIECES)),
        pltpu.SemaphoreType.DMA((nz, PIECES)),
    ]


def gather_kernel(n, x_ref, o_ref, own_sem, *sems):
    me = lax.axis_index("col")
    rows = x_ref.shape[0] // PIECES
    greet("col", n, me)
    own = pltpu.make_async_copy(x_ref, o_ref.at[me], own_sem)
    own.start()
    finish = line_gather(
        n,
        me,
        lambda c: x_ref.at[pl.ds(c * rows, rows)],
        lambda g, c: o_ref.at[g, pl.ds(c * rows, rows)],
        sems,
    )
    own.wait()
    finish()


def row_gather_kernel(n, x_ref, o_ref, send_sem, recv_sem, own_sem):
    me = lax.axis_index("row")
    greet("row", n, me)
    copies = []
    for k in range(1, n):
        peer = lax.rem(me + k, n)
        copies.append(remote(x_ref, o_ref.at[me], send_sem.at[k], recv_sem.at[k], "row", peer))
        copies[-1].start()
    own = pltpu.make_async_copy(x_ref, o_ref.at[me], own_sem)
    own.start()
    own.wait()
    for copy in copies:
        copy.wait()


def add_into(out, rows, terms):
    def step(i, carry):
        at = pl.ds(pl.multiple_of(i * BAND, BAND), BAND)
        total = terms[0](at).astype(F32)
        for term in terms[1:]:
            total = total + term(at).astype(F32)
        out(at, total)
        return carry

    lax.fori_loop(0, rows // BAND, step, 0)


def col_sum_kernel(
    n, x_ref, o_ref, x_buf, z_buf, stage, xs, xr, zs, zr, own_sem, *sems
):
    me = lax.axis_index("col")
    nz = n // 2
    z, x = me // 2, lax.rem(me, 2)
    other = me + 1 - 2 * x
    rows, width = x_ref.shape[0], x_ref.shape[1] // n
    greet("col", n, me)
    order = [lax.rem(z + k, nz) for k in (*range(1, nz), 0)]
    firsts, seconds = [], []
    for to in order:
        src = columns(x_ref, to * 2 + 1 - x, width)
        firsts.append(remote(src, x_buf.at[to], xs.at[to], xr.at[to], "col", other))
        firsts[-1].start()
    for to, first in zip(order[:-1], firsts):
        first.wait_recv()
        mine = pl.ds(pl.multiple_of((to * 2 + x) * width, width), width)

        def put(at, total):
            stage[to, at, :] = total.astype(BF)

        add_into(put, rows, [lambda at: x_ref[at, mine], lambda at: x_buf[to, at, :]])
        seconds.append(remote(stage.at[to], z_buf.at[z], zs.at[to], zr.at[z], "col", to * 2 + x))
        seconds[-1].start()
    firsts[-1].wait_recv()
    for source in order[:-1]:
        block = z_buf.at[source]
        remote(block, block, zs.at[source], zr.at[source], "col", other).wait_recv()
    mine = pl.ds(pl.multiple_of(me * width, width), width)

    def put_own(at, total):
        stage[z, at, :] = total.astype(BF)

    terms = [lambda at: x_ref[at, mine], lambda at: x_buf[z, at, :]]
    for source in order[:-1]:
        terms.append(lambda at, source=source: z_buf[source, at, :])
    add_into(put_own, rows, terms)
    part = rows // PIECES

    def view(g, c):
        return o_ref.at[
            pl.ds(c * part, part), pl.ds(pl.multiple_of(g * width, width), width)
        ]

    own = pltpu.make_async_copy(stage.at[z], columns(o_ref, me, width), own_sem)
    own.start()
    finish = line_gather(n, me, lambda c: stage.at[z, pl.ds(c * part, part)], view, sems)
    own.wait()
    finish()
    for copy in firsts:
        copy.wait_send()
    for copy in seconds:
        copy.wait_send()


def row_sum_kernel(
    n, pieces, x_ref, o_ref, k_buf, y_buf, stage, ks, kr, ys, yr, gs, gr
):
    me = lax.axis_index("row")
    ny = n // 2
    y, k = me // 2, lax.rem(me, 2)
    other = me + 1 - 2 * k
    width = x_ref.shape[1] // 2
    rows = x_ref.shape[0] // pieces
    mine = pl.ds(pl.multiple_of(k * width, width), width)
    theirs = pl.ds(pl.multiple_of((1 - k) * width, width), width)
    greet("row", n, me)
    parts = [pl.ds(c * rows, rows) for c in range(pieces)]
    swaps, sends, hands = [], {}, []
    for c, part in enumerate(parts):
        swaps.append(
            remote(x_ref.at[part, theirs], k_buf.at[part], ks.at[c], kr.at[c], "row", other)
        )
        swaps[-1].start()
    for c, part in enumerate(parts):
        swaps[c].wait_recv()

        def put(at, total, c=c):
            stage[pl.ds(pl.multiple_of(c * rows + at.start, BAND), BAND), :] = total.astype(BF)

        def shifted(at, c=c):
            return pl.ds(pl.multiple_of(c * rows + at.start, BAND), BAND)

        add_into(
            put,
            rows,
            [
                lambda at, s=shifted: x_ref[s(at), mine],
                lambda at, s=shifted: k_buf[s(at), :],
            ],
        )
        for d in range(1, ny):
            peer = lax.rem(y + d, ny) * 2 + k
            sends[c, d] = remote(
                stage.at[part], y_buf.at[d - 1, part], ys.at[d - 1, c], yr.at[d - 1, c], "row", peer
            )
            sends[c, d].start()
    for c, part in enumerate(parts):
        for d in range(1, ny):
            sends[c, d].wait_recv()

        def shifted(at, c=c):
            return pl.ds(pl.multiple_of(c * rows + at.start, BAND), BAND)

        def put(at, total, s=shifted):
            o_ref[s(at), mine] = total.astype(o_ref.dtype)

        terms = [lambda at, s=shifted: stage[s(at), :]]
        for d in range(1, ny):
            terms.append(lambda at, s=shifted, d=d: y_buf[d - 1, s(at), :])
        add_into(put, rows, terms)
        place = o_ref.at[part, mine]
        hands.append(remote(place, place, gs.at[c], gr.at[c], "row", other))
        hands[-1].start()
    for c in range(pieces):
        swaps[c].wait_send()
        for d in range(1, ny):
            sends[c, d].wait_send()
        hands[c].wait()


def launch(kernel, name, number, shape, dtype, scratch, x):
    return pl.pallas_call(
        kernel,
        name=name,
        out_shape=jax.ShapeDtypeStruct(shape, dtype),
        in_specs=[VMEM],
        out_specs=VMEM,
        scratch_shapes=scratch,
        compiler_params=pltpu.CompilerParams(
            collective_id=number, has_side_effects=True, vmem_limit_bytes=44 * 2**20
        ),
    )(x)


def fits(rows, width, n, pieces=PIECES):
    return n % 2 == 0 and rows % (BAND * pieces) == 0 and width % 128 == 0


def gather_col(x, n, number):
    if not fits(*x.shape, n):
        return lax.all_gather(x, "col", axis=0, tiled=True)
    kernel = functools.partial(gather_kernel, n)
    scratch = [pltpu.SemaphoreType.DMA, *gather_sems(n)]
    full = launch(kernel, f"gather{number}", number, (n, *x.shape), x.dtype, scratch, x)
    return full.reshape(n * x.shape[0], x.shape[1])


def gather_row(x, n, number):
    if not fits(*x.shape, n):
        return lax.all_gather(x, "row", axis=0, tiled=True)
    kernel = functools.partial(row_gather_kernel, n)
    sem = pltpu.SemaphoreType.DMA
    scratch = [sem((n,)), sem((n,)), sem]
    full = launch(kernel, f"gather{number}", number, (n, *x.shape), x.dtype, scratch, x)
    return full.reshape(n * x.shape[0], x.shape[1])


def col_sum(x, n, number):
    rows, width = x.shape[0], x.shape[1] // n
    if not fits(rows, width, n):
        return lax.psum(x.astype(F32), "col").astype(BF)
    nz = n // 2
    sem = pltpu.SemaphoreType.DMA
    buf = pltpu.VMEM((nz, rows, width), BF)
    scratch = [buf, buf, buf, *[sem((nz,))] * 4, sem, *gather_sems(n)]
    kernel = functools.partial(col_sum_kernel, n)
    return launch(kernel, f"sum{number}", number, x.shape, BF, scratch, x)


def row_sum(x, n, number):
    rows, width = x.shape[0], x.shape[1] // 2
    if not fits(rows, width, n):
        return lax.psum(x.astype(F32), "row").astype(BF)
    ny = n // 2
    sem = pltpu.SemaphoreType.DMA
    scratch = [
        pltpu.VMEM((rows, width), BF),
        pltpu.VMEM((max(ny - 1, 1), rows, width), BF),
        pltpu.VMEM((rows, width), BF),
        sem((PIECES,)),
        sem((PIECES,)),
        sem((max(ny - 1, 1), PIECES)),
        sem((max(ny - 1, 1), PIECES)),
        sem((PIECES,)),
        sem((PIECES,)),
    ]
    kernel = functools.partial(row_sum_kernel, n, PIECES)
    return launch(kernel, f"sum{number}", number, x.shape, BF, scratch, x)


def factor_kernel(n, size, g_ref, o_ref, slots, work, send_sem, recv_sem):
    me = lax.axis_index("row")
    queries, high, wide = o_ref.shape
    greet("row", n, me)
    copies = []
    for k in range(1, n):
        peer = lax.rem(me + k, n)
        copies.append(
            remote(g_ref, slots.at[me], send_sem.at[k], recv_sem.at[k], "row", peer)
        )
        copies[-1].start()
    slots[me] = g_ref[...]
    for copy in copies:
        copy.wait()
    total = slots[0]
    for k in range(1, n):
        total = total + slots[k]
    work[...] = total
    row = lax.broadcasted_iota(jnp.int32, (high, wide), 0)
    lane = lax.broadcasted_iota(jnp.int32, (high, wide), 1)

    def step(k, carry):
        for q in range(queries):
            t = work[q]
            top = work[q, pl.ds(k, 1), :]
            column = jnp.sum(jnp.where(lane == k, t, 0.0), axis=1, keepdims=True)
            pivot = jnp.sum(jnp.where(lane[:1] == k, top, 0.0), axis=1, keepdims=True)
            part = column / pivot
            top = jnp.where(lane[:1] == k, 0.0, top)
            base = jnp.where(lane == k, 0.0, t)
            moved = jnp.where(lane == k, -part, base - part * top)
            work[q] = jnp.where(row > k, moved, t)
        return carry

    lax.fori_loop(0, size, step, 0)
    for q in range(queries):
        t = work[q]
        diagonal = jnp.sum(jnp.where(lane == row, t, 0.0), axis=1, keepdims=True)
        scale = lax.rsqrt(diagonal)
        scale = scale * (1.5 - 0.5 * diagonal * scale * scale)
        o_ref[q] = jnp.where(lane < row, t * scale, jnp.where(lane == row, scale, 0.0))


def inverse_factor(gram, n, number):
    queries, size, _ = gram.shape
    if n % 2 or size > 128 or size % 8:
        factor = jnp.linalg.cholesky(lax.psum(gram, "row"))
        unit = jnp.broadcast_to(jnp.eye(size, dtype=F32), gram.shape)
        return lax.linalg.triangular_solve(factor, unit, left_side=True, lower=True)
    wide = jnp.pad(gram, ((0, 0), (0, 0), (0, 128 - size)))
    sem = pltpu.SemaphoreType.DMA
    scratch = [pltpu.VMEM((n, *wide.shape), F32), pltpu.VMEM(wide.shape, F32), sem((n,)), sem((n,))]
    kernel = functools.partial(factor_kernel, n, size)
    return launch(kernel, f"factor{number}", number, wide.shape, F32, scratch, wide)[:, :, :size]


def scale_kernel(act_ref, grad_ref, eigen_ref, sketch_ref, scaled_ref, reduced_ref):
    inverse = 1.0 / eigen_ref[...].astype(F32)
    for q in range(act_ref.shape[0]):
        total = lax.dot_general(
            act_ref[q], grad_ref[q], (((0,), (0,)), ((), ())), preferred_element_type=F32
        )
        scaled = (total * inverse).astype(BF)
        scaled_ref[q] = scaled
        part = lax.dot_general(
            sketch_ref[...], scaled, (((1,), (1,)), ((), ())), preferred_element_type=F32
        )
        reduced_ref[q] = part.astype(BF)


def scale_and_reduce(act, grad, eigen, sketch):
    queries, tokens, wide = act.shape
    deep = grad.shape[2]
    size = sketch.shape[0]
    tile = 256
    if wide % tile or deep % 128 or tokens % 8 or size % 8:
        total = jnp.einsum("qtj,qtp->qjp", act, grad, preferred_element_type=F32)
        scaled = (total / eigen.astype(F32)).astype(BF)
        part = jnp.einsum("qjp,sp->qsj", scaled, sketch, preferred_element_type=F32)
        return scaled, part.astype(BF)
    return pl.pallas_call(
        scale_kernel,
        name="scale",
        grid=(wide // tile,),
        in_specs=[
            pl.BlockSpec((queries, tokens, tile), lambda i: (0, 0, i)),
            pl.BlockSpec((queries, tokens, deep), lambda i: (0, 0, 0)),
            pl.BlockSpec((tile, deep), lambda i: (i, 0)),
            pl.BlockSpec((size, deep), lambda i: (0, 0)),
        ],
        out_specs=[
            pl.BlockSpec((queries, tile, deep), lambda i: (0, i, 0)),
            pl.BlockSpec((queries, size, tile), lambda i: (0, 0, i)),
        ],
        out_shape=[
            jax.ShapeDtypeStruct((queries, wide, deep), BF),
            jax.ShapeDtypeStruct((queries, size, wide), BF),
        ],
        compiler_params=pltpu.CompilerParams(vmem_limit_bytes=44 * 2**20),
    )(act, grad, eigen, sketch)


def dot(a, b, contract):
    return lax.dot_general(a, b, ((contract), ((), ())), preferred_element_type=F32)


def on_device(nrow, ncol, acts, grads, basis_in, basis_out, eigen, sketch):
    queries = acts.shape[1]
    size = sketch.shape[0]
    flat = queries * size
    full_grads = gather_row(grads.reshape(-1, grads.shape[2]), nrow, 0)
    rows = full_grads.shape[0]
    tokens = rows // queries
    joined = jnp.concatenate([full_grads, sketch], axis=0)
    joined = jnp.pad(joined, ((0, -joined.shape[0] % (BAND * PIECES)), (0, 0)))
    joined_sum = col_sum(dot(joined, basis_out, ((1,), (0,))).astype(BF), ncol, 1)
    grad_rot = joined_sum[:rows].reshape(tokens, queries, -1).transpose(1, 0, 2)
    sketch_rot = joined_sum[rows : rows + size]
    full_acts = gather_col(acts.reshape(-1, acts.shape[2]), ncol, 2)
    act_rot = row_sum(dot(full_acts, basis_in, ((1,), (0,))).astype(BF), nrow, 3)
    act_rot = act_rot.reshape(tokens, queries, -1).transpose(1, 0, 2)
    scaled, reduced_part = scale_and_reduce(act_rot, grad_rot, eigen, sketch_rot)
    reduced = row_sum(reduced_part.reshape(flat, -1), nrow, 4)
    range_part = dot(reduced, basis_in, ((1,), (1,))).astype(BF)
    range_rows = col_sum(range_part, ncol, 5).reshape(queries, size, -1)
    gram = jnp.einsum("qsi,qri->qsr", range_rows, range_rows, preferred_element_type=F32)
    inverse = inverse_factor(gram, nrow, 6)
    range_basis = jnp.einsum(
        "qsr,qri->qsi", inverse, range_rows.astype(F32), precision=lax.Precision.HIGHEST
    )
    basis_rows = range_basis.astype(BF).reshape(flat, -1)
    mapped = row_sum(dot(basis_rows, basis_in, ((1,), (0,))).astype(BF), nrow, 7)
    mapped = mapped.reshape(queries, size, -1)
    core_part = jnp.einsum("qsj,qjp->qsp", mapped, scaled, preferred_element_type=F32)
    core = col_sum(core_part.astype(BF).reshape(flat, -1), ncol, 8)
    projection_part = dot(core, basis_out, ((1,), (1,))).astype(BF)
    projected = row_sum(projection_part, nrow, 9)
    return range_basis, projected.astype(F32).reshape(queries, size, -1)


def solution(mesh):
    in_specs = (
        P("col", None, "row"),
        P("row", None, "col"),
        P("row", "col"),
        P("col", "row"),
        P("col", "row"),
        P(None, "col"),
    )
    out_specs = (P(None, None, "row"), P(None, None, "col"))
    body = functools.partial(on_device, mesh.shape["row"], mesh.shape["col"])
    return jax.shard_map(body, mesh=mesh, in_specs=in_specs, out_specs=out_specs, check_vma=False)
```

time: 698 us -> 448 us (0.64)
  Pallas kernels: 464 us -> 343 us
  blocking collectives: 53.6 us -> 0 us
  other arithmetic: 44.5 us -> 0.87 us
  matrix products: 123 us -> 89 us
    pallas_call x10, Pallas kernels: 464 us -> 317 us  [launch(): pl.pallas_call(kernel, name=name, out_shape=jax.ShapeDtypeStruct(shape, d...]
    psum x1 -> x0, blocking collectives: 53.6 us -> none  [on_device(): gram = lax.psum(gram_piece, ('row', 'col'))]
    dot_general x9 -> x8, matrix products: 122 us -> 89 us  [the longest x5 72.3 us: dot(): lax.dot_general(a, b, (contract, ((), ())), preferred_element_type=F32)]
    pallas_call x0 -> x1, Pallas kernels: none -> 26.2 us  [scale_and_reduce(): pl.pallas_call(scale_kernel, name='scale', grid=(wide // tile,), in_specs...]
    another operation x7 -> x0, other arithmetic: 24.6 us -> none  [the longest x4 13.4 us: on_device(): factor = jnp.linalg.cholesky(gram)]
    convert_element_type x1 -> x0, other arithmetic: 16.6 us -> none  [on_device(): scaled = (core_sum / eigen.astype(jnp.float32)).astype(bf)]
    reshape x4 -> x6, local copies, waits for them, and re-layouts: 6.06 us -> 13.3 us  [the longest x2 5.48 us: on_device(): grad_rot = joined_sum[:rows].reshape(tokens, queries, -1).transpose(1, 0, 2)]
where the time goes in v1:
time: 448 us
  Pallas kernels  343 us (77%)
  matrix products  89 us (20%)
  local copies, waits for them, and re-layouts  13.5 us (3%)
    pallas_call x10, Pallas kernels, launch(): pl.pallas_call(kernel, name=name, out_shape=jax.ShapeDtypeStruct(shape, d...  317 us
    dot_general x5, matrix products, dot(): lax.dot_general(a, b, (contract, ((), ())), preferred_element_type=F32)  72.3 us
    pallas_call x1, Pallas kernels, scale_and_reduce(): pl.pallas_call(scale_kernel, name='scale', grid=(wide // tile,), in_specs...  26.2 us
    dot_general x1, matrix products, on_device(): jnp.einsum('qsj,qjp->qsp', mapped, scaled, preferred_element_type=F32)  12.3 us

profile of v1, /device:TPU:0, one launch (start us, length us, event | category | flops | bytes accessed | tf_op | source)
XLA Modules:
  0.0 447.6 jit_solution(5213000809223957330)
XLA Ops:
  0.6 1.0 reshape.46.x_ref
  1.7 12.1 %gather0.1 = bf16[4,96,1024]{2,1,0:T(8,128)(2,1)S(1)} custom-call(bf16[96,1024]{1,0:T(8,128)(2,1)S(1)} %reshape.46.x_ref), custom_call_target="tpu_custom_call" | custom-call | tf_op jit(solution)/shard_map/gather0/pallas_call | solution.py:293
  13.8 2.1 reshape.43.x_ref
  15.9 4.4 convolution_convert_fusion.3.x_ref
  20.3 58.7 %sum1.1 = bf16[480,2048]{1,0:T(8,128)(2,1)S(1)} custom-call(bf16[480,2048]{1,0:T(8,128)(2,1)S(1)} %convolution_convert_fusion.3.x_ref), custom_call_target="tpu_custom_call" | custom-call | tf_op jit(solution)/shard_map/sum1/pallas_call | solution.py:293
  79.2 2.3 reshape.48
  81.4 3.2 copy.13
  84.6 62.2 %gather2.1 = bf16[8,48,7168]{2,1,0:T(8,128)(2,1)S(1)} custom-call(bf16[48,7168]{1,0:T(8,128)(2,1)S(1)} %reshape.43.x_ref), custom_call_target="tpu_custom_call" | custom-call | tf_op jit(solution)/shard_map/gather2/pallas_call | solution.py:293
  146.9 25.7 %convolution_convert_fusion.1.x_ref = bf16[384,3584]{1,0:T(8,128)(2,1)S(1)} fusion(bf16[384,7168]{1,0:T(8,128)(2,1)S(1)} %bitcast.34, bf16[7168,3584]{1,0:T(8,128)(2,1)} %param.8), kind=kOutput, calls=%fused_computation.1 | convolution fusion | flops 19731382272 | bytes 59637760 | tf_op jit(solution)/shard_map/dot_general | solution.py:465
  172.6 36.8 %sum3.1 = bf16[384,3584]{1,0:T(8,128)(2,1)S(1)} custom-call(bf16[384,3584]{1,0:T(8,128)(2,1)S(1)} %convolution_convert_fusion.1.x_ref), custom_call_target="tpu_custom_call" | custom-call | tf_op jit(solution)/shard_map/sum3/pallas_call | solution.py:293
  209.4 2.5 reshape.45
  211.9 2.2 copy.12
  214.2 26.2 %scale.1 = (bf16[2,3584,2048]{2,1,0:T(8,128)(2,1)}, bf16[2,72,3584]{2,1,0:T(8,128)(2,1)S(1)}) custom-call(bf16[2,192,3584]{2,1,0:T(8,128)(2,1)S(1)} %bitcast.32, bf16[2,192,2048]{2,1,0:T(8,128)(2,1)S(1)} %bitcast.33, bf16[3584,2048]{1,0:T(8,128)(2,1)} %eigen_ref.1, bf16[72,2048]{1,0:T(8,128)(2,1)S(1)} %slice.10.sketch_ref), custom_call_target="tpu_custom_call" | custom-call | tf_op jit(solution)/shard_map/scale/pallas_call | solution.py:442
  240.4 17.0 %sum4.1 = bf16[144,3584]{1,0:T(8,128)(2,1)S(1)} custom-call(bf16[144,3584]{1,0:T(8,128)(2,1)S(1)} %bitcast.37), custom_call_target="tpu_custom_call" | custom-call | tf_op jit(solution)/shard_map/sum4/pallas_call | solution.py:293
  257.4 22.6 %convolution_convert_fusion.x_ref = bf16[144,7168]{1,0:T(8,128)(2,1)S(1)} fusion(bf16[144,3584]{1,0:T(8,128)(2,1)S(1)} %sum4.1, bf16[7168,3584]{1,0:T(8,128)(2,1)} %param.8), kind=kOutput, calls=%fused_computation | convolution fusion | flops 7399784448 | bytes 54476800 | tf_op jit(solution)/shard_map/dot_general | solution.py:465
  279.9 57.0 %sum5.1 = bf16[144,7168]{1,0:T(8,128)(2,1)S(1)} custom-call(bf16[144,7168]{1,0:T(8,128)(2,1)S(1)} %convolution_convert_fusion.x_ref), custom_call_target="tpu_custom_call" | custom-call | tf_op jit(solution)/shard_map/sum5/pallas_call | solution.py:293
  337.7 19.5 %factor6.1 = f32[2,72,128]{2,1,0:T(8,128)S(1)} custom-call(f32[2,72,128]{2,1,0:T(8,128)S(1)} %pad.9.g_ref), custom_call_target="tpu_custom_call" | custom-call | tf_op jit(solution)/shard_map/factor6/pallas_call | solution.py:293
  357.1 3.8 fusion.14
  360.9 18.1 %convolution_convert_fusion.2.x_ref = bf16[144,3584]{1,0:T(8,128)(2,1)S(1)} fusion(bf16[144,7168]{1,0:T(8,128)(2,1)S(1)} %bitcast.39, bf16[7168,3584]{1,0:T(8,128)(2,1)} %param.8), kind=kOutput, calls=%fused_computation.2 | convolution fusion | flops 7399268352 | bytes 54476800 | tf_op jit(solution)/shard_map/dot_general | solution.py:465
  379.0 17.0 %sum7.1 = bf16[144,3584]{1,0:T(8,128)(2,1)S(1)} custom-call(bf16[144,3584]{1,0:T(8,128)(2,1)S(1)} %convolution_convert_fusion.2.x_ref), custom_call_target="tpu_custom_call" | custom-call | tf_op jit(solution)/shard_map/sum7/pallas_call | solution.py:293
  396.0 12.3 %convolution_convert_fusion.4 = bf16[2,72,2048]{2,1,0:T(8,128)(2,1)S(1)} fusion(bf16[2,72,3584]{2,1,0:T(8,128)(2,1)S(1)} %bitcast.31, bf16[2,3584,2048]{2,1,0:T(8,128)(2,1)} %get-tuple-element.5), kind=kOutput, calls=%fused_computation.5 | convolution fusion | flops 2114224128 | bytes 30982144 | tf_op jit(solution)/shard_map/qsj,qjp->qsp/dot_general | solution.py:495
  408.3 28.5 %sum8.1 = bf16[144,2048]{1,0:T(8,128)(2,1)S(1)} custom-call(bf16[144,2048]{1,0:T(8,128)(2,1)S(1)} %bitcast.35), custom_call_target="tpu_custom_call" | custom-call | tf_op jit(solution)/shard_map/sum8/pallas_call | solution.py:293
  436.7 1.5 convolution_convert_fusion.5.x_ref
  438.3 8.4 %sum9.1 = bf16[144,1024]{1,0:T(8,128)(2,1)S(1)} custom-call(bf16[144,1024]{1,0:T(8,128)(2,1)S(1)} %convolution_convert_fusion.5.x_ref), custom_call_target="tpu_custom_call" | custom-call | tf_op jit(solution)/shard_map/sum9/pallas_call | solution.py:293
  (11 shorter events, 1.8 us)
Async XLA Ops:
  0.6 15.3 %copy-start.2 = (bf16[72,1024]{1,0:T(8,128)(2,1)S(1)}, bf16[72,1024]{1,0:T(8,128)(2,1)}, u32[]{:S(2)}) copy-start(bf16[72,1024]{1,0:T(8,128)(2,1)} %param.11) | copy-start | bytes 442372
  211.9 2.2 copy-start
  396.0 40.8 %copy-start.1 = (bf16[1024,2048]{1,0:T(8,128)(2,1)S(1)}, bf16[1024,2048]{1,0:T(8,128)(2,1)}, u32[]{:S(2)}) copy-start(bf16[1024,2048]{1,0:T(8,128)(2,1)} %param.9) | copy-start | bytes 12582916

commit v2 on v1

--- a/solution.py
+++ b/solution.py
@@ -10,6 +10,11 @@
 VMEM = pl.BlockSpec(memory_space=pltpu.VMEM)
 BAND = 16
 PIECES = 3
+TILE = 256
+DEPTH = 3
+LAG = 4
+GAP = 3
+ANY = pl.BlockSpec(memory_space=pl.ANY)
 BF = jnp.bfloat16
 F32 = jnp.float32
 
@@ -72,28 +77,29 @@
 
         across(z, c, own(c)).start()
 
-    for d in range(1, nz):
-        for c in range(PIECES):
-
-            @pl.when(z >= d)
-            def _():
-                block = arrived(z - d, c)
-
-                @pl.when(z < nz - 1)
+    def relay():
+        for d in range(1, nz):
+            for c in range(PIECES):
+
+                @pl.when(z >= d)
                 def _():
-                    along(1, z - d, c, block).start()
-
-                across(z - d, c, block).start()
-
-            @pl.when(z + d < nz)
-            def _():
-                block = arrived(z + d, c)
-
-                @pl.when(z > 0)
+                    block = arrived(z - d, c)
+
+                    @pl.when(z < nz - 1)
+                    def _():
+                        along(1, z - d, c, block).start()
+
+                    across(z - d, c, block).start()
+
+                @pl.when(z + d < nz)
                 def _():
-                    along(-1, z + d, c, block).start()
-
-                across(z + d, c, block).start()
+                    block = arrived(z + d, c)
+
+                    @pl.when(z > 0)
+                    def _():
+                        along(-1, z + d, c, block).start()
+
+                    across(z + d, c, block).start()
 
     def finish():
         for o in range(nz):
@@ -110,7 +116,7 @@
                 def _():
                     along(-1, o, c, view(o * 2 + x, c)).wait_send()
 
-    return finish
+    return relay, finish
 
 
 def gather_sems(n):
@@ -123,36 +129,47 @@
     ]
 
 
-def gather_kernel(n, x_ref, o_ref, own_sem, *sems):
-    me = lax.axis_index("col")
+def gather_both_kernel(
+    ncol, nrow, x_ref, g_ref, o_ref, p_ref, own_sem, send_sem, recv_sem, own_two, *sems
+):
+    me, mine = lax.axis_index("col"), lax.axis_index("row")
     rows = x_ref.shape[0] // PIECES
-    greet("col", n, me)
-    own = pltpu.make_async_copy(x_ref, o_ref.at[me], own_sem)
-    own.start()
-    finish = line_gather(
-        n,
+    greet_both(ncol, nrow, me, mine)
+    relay, finish = line_gather(
+        ncol,
         me,
         lambda c: x_ref.at[pl.ds(c * rows, rows)],
         lambda g, c: o_ref.at[g, pl.ds(c * rows, rows)],
         sems,
     )
-    own.wait()
-    finish()
-
-
-def row_gather_kernel(n, x_ref, o_ref, send_sem, recv_sem, own_sem):
-    me = lax.axis_index("row")
-    greet("row", n, me)
     copies = []
-    for k in range(1, n):
-        peer = lax.rem(me + k, n)
-        copies.append(remote(x_ref, o_ref.at[me], send_sem.at[k], recv_sem.at[k], "row", peer))
+    for k in range(1, nrow):
+        peer = lax.rem(mine + k, nrow)
+        copies.append(remote(g_ref, p_ref.at[mine], send_sem.at[k], recv_sem.at[k], "row", peer))
         copies[-1].start()
     own = pltpu.make_async_copy(x_ref, o_ref.at[me], own_sem)
     own.start()
+    two = pltpu.make_async_copy(g_ref, p_ref.at[mine], own_two)
+    two.start()
     own.wait()
+    two.wait()
+    relay()
+    finish()
     for copy in copies:
         copy.wait()
+
+
+def greet_both(ncol, nrow, me, mine):
+    barrier = pltpu.get_barrier_semaphore()
+    for k in range(1, ncol):
+        pl.semaphore_signal(
+            barrier, inc=1, device_id={"col": lax.rem(me + k, ncol)}, device_id_type=MESH
+        )
+    for k in range(1, nrow):
+        pl.semaphore_signal(
+            barrier, inc=1, device_id={"row": lax.rem(mine + k, nrow)}, device_id_type=MESH
+        )
+    pl.semaphore_wait(barrier, ncol + nrow - 2)
 
 
 def add_into(out, rows, terms):
@@ -167,60 +184,219 @@
     lax.fori_loop(0, rows // BAND, step, 0)
 
 
-def col_sum_kernel(
-    n, x_ref, o_ref, x_buf, z_buf, stage, xs, xr, zs, zr, own_sem, *sems
+def col_sum_stages(
+    n, me, x_ref, o_ref, x_buf, z_buf, stage, xs, xr, zs, zr, own_sem, *sems
 ):
-    me = lax.axis_index("col")
     nz = n // 2
     z, x = me // 2, lax.rem(me, 2)
     other = me + 1 - 2 * x
     rows, width = x_ref.shape[0], x_ref.shape[1] // n
-    greet("col", n, me)
+    part = rows // PIECES
     order = [lax.rem(z + k, nz) for k in (*range(1, nz), 0)]
-    firsts, seconds = [], []
-    for to in order:
+
+    def first(to):
         src = columns(x_ref, to * 2 + 1 - x, width)
-        firsts.append(remote(src, x_buf.at[to], xs.at[to], xr.at[to], "col", other))
-        firsts[-1].start()
-    for to, first in zip(order[:-1], firsts):
-        first.wait_recv()
+        return remote(src, x_buf.at[to], xs.at[to], xr.at[to], "col", other)
+
+    def second(to):
+        return remote(stage.at[to], z_buf.at[z], zs.at[to], zr.at[z], "col", to * 2 + x)
+
+    def begin():
+        for to in order:
+            first(to).start()
+
+    def pair(to):
+        first(to).wait_recv()
         mine = pl.ds(pl.multiple_of((to * 2 + x) * width, width), width)
 
         def put(at, total):
             stage[to, at, :] = total.astype(BF)
 
         add_into(put, rows, [lambda at: x_ref[at, mine], lambda at: x_buf[to, at, :]])
-        seconds.append(remote(stage.at[to], z_buf.at[z], zs.at[to], zr.at[z], "col", to * 2 + x))
-        seconds[-1].start()
-    firsts[-1].wait_recv()
-    for source in order[:-1]:
-        block = z_buf.at[source]
-        remote(block, block, zs.at[source], zr.at[source], "col", other).wait_recv()
-    mine = pl.ds(pl.multiple_of(me * width, width), width)
-
-    def put_own(at, total):
-        stage[z, at, :] = total.astype(BF)
-
-    terms = [lambda at: x_ref[at, mine], lambda at: x_buf[z, at, :]]
-    for source in order[:-1]:
-        terms.append(lambda at, source=source: z_buf[source, at, :])
-    add_into(put_own, rows, terms)
-    part = rows // PIECES
+        second(to).start()
 
     def view(g, c):
         return o_ref.at[
             pl.ds(c * part, part), pl.ds(pl.multiple_of(g * width, width), width)
         ]
 
-    own = pltpu.make_async_copy(stage.at[z], columns(o_ref, me, width), own_sem)
-    own.start()
-    finish = line_gather(n, me, lambda c: stage.at[z, pl.ds(c * part, part)], view, sems)
-    own.wait()
+    def gather():
+        return line_gather(n, me, lambda c: stage.at[z, pl.ds(c * part, part)], view, sems)
+
+    def total():
+        first(z).wait_recv()
+        for source in order[:-1]:
+            block = z_buf.at[source]
+            remote(block, block, zs.at[source], zr.at[source], "col", other).wait_recv()
+        mine = pl.ds(pl.multiple_of(me * width, width), width)
+
+        def put(at, value):
+            stage[z, at, :] = value.astype(BF)
+
+        terms = [lambda at: x_ref[at, mine], lambda at: x_buf[z, at, :]]
+        for source in order[:-1]:
+            terms.append(lambda at, source=source: z_buf[source, at, :])
+        add_into(put, rows, terms)
+        own = pltpu.make_async_copy(stage.at[z], columns(o_ref, me, width), own_sem)
+        own.start()
+        relay, finish = gather()
+        own.wait()
+        relay()
+        finish()
+        for to in order:
+            first(to).wait_send()
+        for to in order[:-1]:
+            second(to).wait_send()
+
+    return [begin, *[functools.partial(pair, to) for to in order[:-1]], total]
+
+
+def col_sum_kernel(n, *refs):
+    me = lax.axis_index("col")
+    greet("col", n, me)
+    for stage in col_sum_stages(n, me, *refs):
+        stage()
+
+
+def col_sum_scratch(n, rows, width):
+    nz = n // 2
+    sem = pltpu.SemaphoreType.DMA
+    buf = pltpu.VMEM((nz, rows, width), BF)
+    return [buf, buf, buf, *[sem((nz,))] * 4, sem, *gather_sems(n)]
+
+
+def tile_sum(me, count, tile, part, o_ref, k_buf, y_buf, stage, ks, kr, ys, yr, gs, gr):
+    y, k = me // 2, lax.rem(me, 2)
+    other = me + 1 - 2 * k
+    across = (1 - y) * 2 + k
+    half = tile // 2
+    mine = pl.ds(pl.multiple_of(k * half, half), half)
+    theirs = pl.ds(pl.multiple_of((1 - k) * half, half), half)
+
+    def spot(i):
+        return pl.ds(pl.multiple_of(i * tile + k * half, half), half)
+
+    def swap(i):
+        return remote(part.at[i, :, theirs], k_buf.at[i], ks.at[i], kr.at[i], "row", other)
+
+    def cross(i):
+        return remote(stage.at[i], y_buf.at[i], ys.at[i], yr.at[i], "row", across)
+
+    def hand(i):
+        place = o_ref.at[:, spot(i)]
+        return remote(place, place, gs.at[i], gr.at[i], "row", other)
+
+    def middle(i):
+        swap(i).wait_recv()
+        stage[i] = (part[i, :, mine].astype(F32) + k_buf[i].astype(F32)).astype(BF)
+        cross(i).start()
+
+    def last(i):
+        cross(i).wait_recv()
+        o_ref[:, spot(i)] = (stage[i].astype(F32) + y_buf[i].astype(F32)).astype(BF)
+        hand(i).start()
+
+    def finish():
+        def step(i, carry):
+            swap(i).wait_send()
+            cross(i).wait_send()
+            hand(i).wait()
+            return carry
+
+        lax.fori_loop(0, count, step, 0)
+
+    return swap, middle, last, finish
+
+
+def tile_scratch(count, rows, tile):
+    sem = pltpu.SemaphoreType.DMA
+    half = pltpu.VMEM((count, rows, tile // 2), BF)
+    return [pltpu.VMEM((count, rows, tile), BF), half, half, half, *[sem((count,))] * 6]
+
+
+def tile_loop(count, compute, swap, middle, last, hooks):
+    def step(i, carry):
+        @pl.when(i < count)
+        def _():
+            compute(i)
+            swap(i).start()
+
+        @pl.when((i >= 1) & (i <= count))
+        def _():
+            middle(i - 1)
+
+        @pl.when(i >= LAG)
+        def _():
+            last(i - LAG)
+
+        for at, hook in hooks:
+            pl.when(i == at)(hook)
+        return carry
+
+    lax.fori_loop(0, count + LAG, step, 0)
+
+
+def stream_parts(n, me, a_ref, w_ref, o_ref, w_buf, w_sem, part, *rest):
+    tile = w_buf.shape[2]
+    count = w_ref.shape[1] // tile
+
+    def fetch(i):
+        at = pl.ds(pl.multiple_of(i * tile, tile), tile)
+        slot = lax.rem(i, DEPTH)
+        return pltpu.make_async_copy(w_ref.at[:, at], w_buf.at[slot], w_sem.at[slot])
+
+    def compute(i):
+        fetch(i).wait()
+
+        @pl.when(i + DEPTH - 1 < count)
+        def _():
+            fetch(i + DEPTH - 1).start()
+
+        product = jnp.dot(a_ref[...], w_buf[lax.rem(i, DEPTH)], preferred_element_type=F32)
+        part[i] = product.astype(BF)
+
+    for i in range(min(DEPTH - 1, count)):
+        fetch(i).start()
+    return count, compute, tile_sum(me, count, tile, part, o_ref, *rest)
+
+
+def stream_scratch(count, rows, deep, tile):
+    return [
+        pltpu.VMEM((DEPTH, deep, tile), BF),
+        pltpu.SemaphoreType.DMA((DEPTH,)),
+        *tile_scratch(count, rows, tile),
+    ]
+
+
+def stream_kernel(n, a_ref, w_ref, o_ref, *scratch):
+    me = lax.axis_index("row")
+    count, compute, (swap, middle, last, finish) = stream_parts(
+        n, me, a_ref, w_ref, o_ref, *scratch
+    )
+    greet("row", n, me)
+    tile_loop(count, compute, swap, middle, last, [])
     finish()
-    for copy in firsts:
-        copy.wait_send()
-    for copy in seconds:
-        copy.wait_send()
+
+
+STREAM = 12
+
+
+def stream_both_kernel(n, ncol, a_ref, w_ref, x_ref, o_ref, s_ref, *scratch):
+    me, mine = lax.axis_index("row"), lax.axis_index("col")
+    count, compute, (swap, middle, last, finish) = stream_parts(
+        n, me, a_ref, w_ref, o_ref, *scratch[:STREAM]
+    )
+    greet_both(ncol, n, mine, me)
+    begin, *pairs, total = col_sum_stages(ncol, mine, x_ref, s_ref, *scratch[STREAM:])
+    begin()
+    hooks = [(GAP * (k + 1), pair) for k, pair in enumerate(pairs)]
+    late = [pair for at, pair in hooks if at >= count + LAG]
+    hooks = [hook for hook in hooks if hook[0] < count + LAG]
+    tile_loop(count, compute, swap, middle, last, hooks)
+    for pair in late:
+        pair()
+    total()
+    finish()
 
 
 def row_sum_kernel(
@@ -289,51 +465,89 @@
         hands[c].wait()
 
 
-def launch(kernel, name, number, shape, dtype, scratch, x):
+def launch(kernel, name, number, shape, dtype, scratch, *args, specs=None, outs=None, more=None):
+    out = jax.ShapeDtypeStruct(shape, dtype)
     return pl.pallas_call(
         kernel,
         name=name,
-        out_shape=jax.ShapeDtypeStruct(shape, dtype),
-        in_specs=[VMEM],
-        out_specs=VMEM,
+        out_shape=out if more is None else [out, more],
+        in_specs=specs or [VMEM] * len(args),
+        out_specs=outs or (VMEM if more is None else [VMEM, VMEM]),
         scratch_shapes=scratch,
         compiler_params=pltpu.CompilerParams(
-            collective_id=number, has_side_effects=True, vmem_limit_bytes=44 * 2**20
+            collective_id=number, has_side_effects=True, vmem_limit_bytes=48 * 2**20
         ),
-    )(x)
+    )(*args)
 
 
 def fits(rows, width, n, pieces=PIECES):
     return n % 2 == 0 and rows % (BAND * pieces) == 0 and width % 128 == 0
 
 
-def gather_col(x, n, number):
-    if not fits(*x.shape, n):
-        return lax.all_gather(x, "col", axis=0, tiled=True)
-    kernel = functools.partial(gather_kernel, n)
-    scratch = [pltpu.SemaphoreType.DMA, *gather_sems(n)]
-    full = launch(kernel, f"gather{number}", number, (n, *x.shape), x.dtype, scratch, x)
-    return full.reshape(n * x.shape[0], x.shape[1])
-
-
-def gather_row(x, n, number):
-    if not fits(*x.shape, n):
-        return lax.all_gather(x, "row", axis=0, tiled=True)
-    kernel = functools.partial(row_gather_kernel, n)
+def gather_both(acts, grads, nrow, ncol, number):
+    if not (fits(*acts.shape, ncol) and fits(*grads.shape, nrow)):
+        full = lax.all_gather(acts, "col", axis=0, tiled=True)
+        return full, lax.all_gather(grads, "row", axis=0, tiled=True)
     sem = pltpu.SemaphoreType.DMA
-    scratch = [sem((n,)), sem((n,)), sem]
-    full = launch(kernel, f"gather{number}", number, (n, *x.shape), x.dtype, scratch, x)
-    return full.reshape(n * x.shape[0], x.shape[1])
+    scratch = [sem, sem((nrow,)), sem((nrow,)), sem, *gather_sems(ncol)]
+    full, part = launch(
+        functools.partial(gather_both_kernel, ncol, nrow),
+        f"gather{number}",
+        number,
+        (ncol, *acts.shape),
+        BF,
+        scratch,
+        acts,
+        grads,
+        more=jax.ShapeDtypeStruct((nrow, *grads.shape), BF),
+    )
+    return full.reshape(-1, acts.shape[1]), part.reshape(-1, grads.shape[1])
+
+
+def streams(a, w, n):
+    return n == 4 and a.shape[0] % BAND == 0 and a.shape[1] % 128 == 0 and w.shape[1] % TILE == 0
+
+
+def dot_row_sum(a, w, n, number):
+    if not streams(a, w, n):
+        return row_sum(dot(a, w, ((1,), (0,))).astype(BF), n, number)
+    rows, wide = a.shape[0], w.shape[1]
+    scratch = stream_scratch(wide // TILE, rows, a.shape[1], TILE)
+    kernel = functools.partial(stream_kernel, n)
+    return launch(
+        kernel, f"stream{number}", number, (rows, wide), BF, scratch, a, w, specs=[VMEM, ANY]
+    )
+
+
+def dot_both_sums(a, w, x, nrow, ncol, number):
+    if not (streams(a, w, nrow) and fits(x.shape[0], x.shape[1] // ncol, ncol)):
+        act = row_sum(dot(a, w, ((1,), (0,))).astype(BF), nrow, number)
+        return act, col_sum(x, ncol, number + 20)
+    rows, wide = a.shape[0], w.shape[1]
+    scratch = [
+        *stream_scratch(wide // TILE, rows, a.shape[1], TILE),
+        *col_sum_scratch(ncol, x.shape[0], x.shape[1] // ncol),
+    ]
+    return launch(
+        functools.partial(stream_both_kernel, nrow, ncol),
+        f"stream{number}",
+        number,
+        (rows, wide),
+        BF,
+        scratch,
+        a,
+        w,
+        x,
+        specs=[VMEM, ANY, VMEM],
+        more=jax.ShapeDtypeStruct(x.shape, BF),
+    )
 
 
 def col_sum(x, n, number):
     rows, width = x.shape[0], x.shape[1] // n
     if not fits(rows, width, n):
         return lax.psum(x.astype(F32), "col").astype(BF)
-    nz = n // 2
-    sem = pltpu.SemaphoreType.DMA
-    buf = pltpu.VMEM((nz, rows, width), BF)
-    scratch = [buf, buf, buf, *[sem((nz,))] * 4, sem, *gather_sems(n)]
+    scratch = col_sum_scratch(n, rows, width)
     kernel = functools.partial(col_sum_kernel, n)
     return launch(kernel, f"sum{number}", number, x.shape, BF, scratch, x)
 
@@ -415,50 +629,117 @@
     return launch(kernel, f"factor{number}", number, wide.shape, F32, scratch, wide)[:, :, :size]
 
 
-def scale_kernel(act_ref, grad_ref, eigen_ref, sketch_ref, scaled_ref, reduced_ref):
-    inverse = 1.0 / eigen_ref[...].astype(F32)
-    for q in range(act_ref.shape[0]):
-        total = lax.dot_general(
-            act_ref[q], grad_ref[q], (((0,), (0,)), ((), ())), preferred_element_type=F32
-        )
-        scaled = (total * inverse).astype(BF)
-        scaled_ref[q] = scaled
-        part = lax.dot_general(
-            sketch_ref[...], scaled, (((1,), (1,)), ((), ())), preferred_element_type=F32
-        )
-        reduced_ref[q] = part.astype(BF)
-
-
-def scale_and_reduce(act, grad, eigen, sketch):
-    queries, tokens, wide = act.shape
-    deep = grad.shape[2]
+def query_rows(value, q, queries, blocks):
+    rows, wide = value.shape
+    split = value.astype(F32).reshape(blocks, queries, rows // (blocks * queries), wide)
+    return split[:, q].reshape(rows // queries, wide).astype(BF)
+
+
+def scale_kernel(
+    n, blocks, queries, act_ref, grad_ref, sketch_ref, eigen_ref, scaled_ref, o_ref,
+    grad_buf, e_buf, s_buf, e_sem, s_sem, part, *rest,
+):
+    me = lax.axis_index("row")
+    tile = e_buf.shape[1]
+    count = eigen_ref.shape[0] // tile
+    size = sketch_ref.shape[0]
+    swap, middle, last, finish = tile_sum(me, count, tile, part, o_ref, *rest)
+
+    def fetch(i):
+        at = pl.ds(pl.multiple_of(i * tile, tile), tile)
+        slot = lax.rem(i, DEPTH)
+        return pltpu.make_async_copy(eigen_ref.at[at], e_buf.at[slot], e_sem.at[slot])
+
+    def store(i):
+        at = pl.ds(pl.multiple_of(i * tile, tile), tile)
+        slot = lax.rem(i, 2)
+        return pltpu.make_async_copy(s_buf.at[slot], scaled_ref.at[:, at], s_sem.at[slot])
+
+    for i in range(min(DEPTH - 1, count)):
+        fetch(i).start()
+    for q in range(queries):
+        for c in range(grad_ref.shape[1] // tile):
+            at = pl.ds(c * tile, tile)
+            grad_buf[q, :, at] = query_rows(grad_ref[:, at], q, queries, blocks[1])
+    greet("row", n, me)
+
+    def compute(i):
+        fetch(i).wait()
+
+        @pl.when(i + DEPTH - 1 < count)
+        def _():
+            fetch(i + DEPTH - 1).start()
+
+        @pl.when(i >= 2)
+        def _():
+            store(i - 2).wait()
+
+        slot = lax.rem(i, 2)
+        inverse = 1.0 / e_buf[lax.rem(i, DEPTH)].astype(F32)
+        act = act_ref[:, pl.ds(pl.multiple_of(i * tile, tile), tile)]
+        pieces = []
+        for q in range(queries):
+            total = lax.dot_general(
+                query_rows(act, q, queries, blocks[0]),
+                grad_buf[q],
+                (((0,), (0,)), ((), ())),
+                preferred_element_type=F32,
+            )
+            scaled = (total * inverse).astype(BF)
+            s_buf[slot, q] = scaled
+            pieces.append(
+                lax.dot_general(
+                    sketch_ref[...], scaled, (((1,), (1,)), ((), ())), preferred_element_type=F32
+                )
+            )
+        part[i] = jnp.concatenate(pieces, axis=0).astype(BF)
+        store(i).start()
+
+    tile_loop(count, compute, swap, middle, last, [])
+    finish()
+    for i in range(max(count - 2, 0), count):
+        store(i).wait()
+
+
+def scale_and_reduce(act, grad, eigen, sketch, queries, blocks, n, number):
+    rows, wide = act.shape
+    deep = grad.shape[1]
     size = sketch.shape[0]
-    tile = 256
-    if wide % tile or deep % 128 or tokens % 8 or size % 8:
+    ok = n == 4 and wide % TILE == 0 and deep % TILE == 0 and size % 8 == 0
+    ok = ok and queries * size % BAND == 0 and rows // queries % BAND == 0
+    if not (ok and all(rows % (8 * queries * b) == 0 for b in blocks)):
+        act = act.reshape(blocks[0], queries, -1, wide)
+        grad = grad.reshape(blocks[1], queries, -1, deep)
+        act = act.transpose(1, 0, 2, 3).reshape(queries, -1, wide)
+        grad = grad.transpose(1, 0, 2, 3).reshape(queries, -1, deep)
         total = jnp.einsum("qtj,qtp->qjp", act, grad, preferred_element_type=F32)
         scaled = (total / eigen.astype(F32)).astype(BF)
         part = jnp.einsum("qjp,sp->qsj", scaled, sketch, preferred_element_type=F32)
-        return scaled, part.astype(BF)
-    return pl.pallas_call(
-        scale_kernel,
-        name="scale",
-        grid=(wide // tile,),
-        in_specs=[
-            pl.BlockSpec((queries, tokens, tile), lambda i: (0, 0, i)),
-            pl.BlockSpec((queries, tokens, deep), lambda i: (0, 0, 0)),
-            pl.BlockSpec((tile, deep), lambda i: (i, 0)),
-            pl.BlockSpec((size, deep), lambda i: (0, 0)),
-        ],
-        out_specs=[
-            pl.BlockSpec((queries, tile, deep), lambda i: (0, i, 0)),
-            pl.BlockSpec((queries, size, tile), lambda i: (0, 0, i)),
-        ],
-        out_shape=[
-            jax.ShapeDtypeStruct((queries, wide, deep), BF),
-            jax.ShapeDtypeStruct((queries, size, wide), BF),
-        ],
-        compiler_params=pltpu.CompilerParams(vmem_limit_bytes=44 * 2**20),
-    )(act, grad, eigen, sketch)
+        return scaled, row_sum(part.astype(BF).reshape(queries * size, wide), n, number)
+    sem = pltpu.SemaphoreType.DMA
+    scratch = [
+        pltpu.VMEM((queries, rows // queries, deep), BF),
+        pltpu.VMEM((DEPTH, TILE, deep), BF),
+        pltpu.VMEM((2, queries, TILE, deep), BF),
+        sem((DEPTH,)),
+        sem((2,)),
+        *tile_scratch(wide // TILE, queries * size, TILE),
+    ]
+    return launch(
+        functools.partial(scale_kernel, n, blocks, queries),
+        f"scale{number}",
+        number,
+        (queries, wide, deep),
+        BF,
+        scratch,
+        act,
+        grad,
+        sketch,
+        eigen,
+        specs=[VMEM, VMEM, VMEM, ANY],
+        outs=[ANY, VMEM],
+        more=jax.ShapeDtypeStruct((queries * size, wide), BF),
+    )
 
 
 def dot(a, b, contract):
@@ -469,19 +750,22 @@
     queries = acts.shape[1]
     size = sketch.shape[0]
     flat = queries * size
-    full_grads = gather_row(grads.reshape(-1, grads.shape[2]), nrow, 0)
+    full_acts, full_grads = gather_both(
+        acts.transpose(1, 0, 2).reshape(-1, acts.shape[2]),
+        grads.transpose(1, 0, 2).reshape(-1, grads.shape[2]),
+        nrow,
+        ncol,
+        0,
+    )
     rows = full_grads.shape[0]
-    tokens = rows // queries
     joined = jnp.concatenate([full_grads, sketch], axis=0)
     joined = jnp.pad(joined, ((0, -joined.shape[0] % (BAND * PIECES)), (0, 0)))
-    joined_sum = col_sum(dot(joined, basis_out, ((1,), (0,))).astype(BF), ncol, 1)
-    grad_rot = joined_sum[:rows].reshape(tokens, queries, -1).transpose(1, 0, 2)
-    sketch_rot = joined_sum[rows : rows + size]
-    full_acts = gather_col(acts.reshape(-1, acts.shape[2]), ncol, 2)
-    act_rot = row_sum(dot(full_acts, basis_in, ((1,), (0,))).astype(BF), nrow, 3)
-    act_rot = act_rot.reshape(tokens, queries, -1).transpose(1, 0, 2)
-    scaled, reduced_part = scale_and_reduce(act_rot, grad_rot, eigen, sketch_rot)
-    reduced = row_sum(reduced_part.reshape(flat, -1), nrow, 4)
+    joined_part = dot(joined, basis_out, ((1,), (0,))).astype(BF)
+    act_rot, joined_sum = dot_both_sums(full_acts, basis_in, joined_part, nrow, ncol, 1)
+    grad_rot, sketch_rot = joined_sum[:rows], joined_sum[rows : rows + size]
+    scaled, reduced = scale_and_reduce(
+        act_rot, grad_rot, eigen, sketch_rot, queries, (ncol, nrow), nrow, 2
+    )
     range_part = dot(reduced, basis_in, ((1,), (1,))).astype(BF)
     range_rows = col_sum(range_part, ncol, 5).reshape(queries, size, -1)
     gram = jnp.einsum("qsi,qri->qsr", range_rows, range_rows, preferred_element_type=F32)
@@ -490,7 +774,7 @@
         "qsr,qri->qsi", inverse, range_rows.astype(F32), precision=lax.Precision.HIGHEST
     )
     basis_rows = range_basis.astype(BF).reshape(flat, -1)
-    mapped = row_sum(dot(basis_rows, basis_in, ((1,), (0,))).astype(BF), nrow, 7)
+    mapped = dot_row_sum(basis_rows, basis_in, nrow, 7)
     mapped = mapped.reshape(queries, size, -1)
     core_part = jnp.einsum("qsj,qjp->qsp", mapped, scaled, preferred_element_type=F32)
     core = col_sum(core_part.astype(BF).reshape(flat, -1), ncol, 8)

time: 448 us -> 350 us (0.78)
  Pallas kernels: 343 us -> 299 us
  matrix products: 89 us -> 45.2 us
  local copies, waits for them, and re-layouts: 13.5 us -> 3.99 us
    pallas_call x11 -> x8, Pallas kernels: 343 us -> 299 us  [launch(): pl.pallas_call(kernel, name=name, out_shape=out if more is None else [out...]
    dot_general x5 -> x3, matrix products: 72.3 us -> 28.5 us  [dot(): lax.dot_general(a, b, (contract, ((), ())), preferred_element_type=F32)]
    reshape x6 -> x0, local copies, waits for them, and re-layouts: 13.3 us -> none  [the longest x2 5.48 us: on_device(): grad_rot = joined_sum[:rows].reshape(tokens, queries, -1).transpose(1, 0, 2)]
where the time goes in v2:
time: 350 us
  Pallas kernels  299 us (85%)
  matrix products  45.2 us (13%)
  local copies, waits for them, and re-layouts  3.99 us (1%)
    pallas_call x8, Pallas kernels, launch(): pl.pallas_call(kernel, name=name, out_shape=out if more is None else [out...  299 us
    dot_general x3, matrix products, dot(): lax.dot_general(a, b, (contract, ((), ())), preferred_element_type=F32)  28.5 us
    dot_general x1, matrix products, on_device(): jnp.einsum('qsj,qjp->qsp', mapped, scaled, preferred_element_type=F32)  12.3 us

profile of v2, /device:TPU:0, one launch (start us, length us, event | category | flops | bytes accessed | tf_op | source)
XLA Modules:
  0.0 349.7 jit_solution(14980302560833680028)
XLA Ops:
  0.6 0.0 copy-start.2
  0.6 1.0 copy.9
  1.6 1.2 copy.8
  2.9 69.0 %gather0.1 = (bf16[8,48,7168]{2,1,0:T(8,128)(2,1)}, bf16[4,96,1024]{2,1,0:T(8,128)(2,1)S(1)}) custom-call(bf16[48,7168]{1,0:T(8,128)(2,1)S(1)} %bitcast.27, bf16[96,1024]{1,0:T(8,128)(2,1)S(1)} %bitcast.29), custom_call_target="tpu_custom_call" | custom-call | tf_op jit(solution)/shard_map/gather0/pallas_call | solution.py:470
  71.9 0.0 copy-done.2
  71.9 4.4 %convolution_convert_fusion.1.x_ref = bf16[480,2048]{1,0:T(8,128)(2,1)S(1)} fusion(bf16[1024,2048]{1,0:T(8,128)(2,1)} %param.9, bf16[72,1024]{1,0:T(8,128)(2,1)S(1)} %copy-done.2, bf16[384,1024]{1,0:T(8,128)(2,1)S(1)} %bitcast.30), kind=kOutput, calls=%fused_computation.1 | convolution fusion | flops 2017689600 | bytes 7094272 | tf_op jit(solution)/shard_map/dot_general | solution.py:746
  76.3 66.0 %stream1.1 = (bf16[384,3584]{1,0:T(8,128)(2,1)}, bf16[480,2048]{1,0:T(8,128)(2,1)S(1)}) custom-call(bf16[384,7168]{1,0:T(8,128)(2,1)} %bitcast.31, bf16[7168,3584]{1,0:T(8,128)(2,1)} %w_ref.3, bf16[480,2048]{1,0:T(8,128)(2,1)S(1)} %convolution_convert_fusion.1.x_ref), custom_call_target="tpu_custom_call" | custom-call | tf_op jit(solution)/shard_map/stream1/pallas_call | solution.py:470
  142.3 0.0 copy-start
  142.3 0.2 slice.9.grad_ref
  142.5 1.6 copy-done
  144.1 27.0 %scale2.1 = (bf16[2,3584,2048]{2,1,0:T(8,128)(2,1)}, bf16[144,3584]{1,0:T(8,128)(2,1)S(1)}) custom-call(bf16[384,3584]{1,0:T(8,128)(2,1)S(1)} %copy-done, bf16[384,2048]{1,0:T(8,128)(2,1)S(1)} %slice.9.grad_ref, bf16[72,2048]{1,0:T(8,128)(2,1)S(1)} %slice.10.sketch_ref, bf16[3584,2048]{1,0:T(8,128)(2,1)} %eigen_ref.1), custom_call_target="tpu_custom_call" | custom-call | tf_op jit(solution)/shard_map/scale2/pallas_call | solution.py:470
  171.1 22.6 %convolution_convert_fusion.refs_0_ = bf16[144,7168]{1,0:T(8,128)(2,1)S(1)} fusion(bf16[144,3584]{1,0:T(8,128)(2,1)S(1)} %get-tuple-element.12, bf16[7168,3584]{1,0:T(8,128)(2,1)} %w_ref.3), kind=kOutput, calls=%fused_computation | convolution fusion | flops 7399784448 | bytes 54476800 | tf_op jit(solution)/shard_map/dot_general | solution.py:746
  193.7 57.1 %sum5.1 = bf16[144,7168]{1,0:T(8,128)(2,1)S(1)} custom-call(bf16[144,7168]{1,0:T(8,128)(2,1)S(1)} %convolution_convert_fusion.refs_0_), custom_call_target="tpu_custom_call" | custom-call | tf_op jit(solution)/shard_map/sum5/pallas_call | solution.py:470
  250.8 0.7 fusion.15
  251.5 19.3 %factor6.1 = f32[2,72,128]{2,1,0:T(8,128)S(1)} custom-call(f32[2,72,128]{2,1,0:T(8,128)S(1)} %pad.9.g_ref), custom_call_target="tpu_custom_call" | custom-call | tf_op jit(solution)/shard_map/factor6/pallas_call | solution.py:470
  270.8 3.8 %fusion.14 = (bf16[2,72,7168]{2,1,0:T(8,128)(2,1)S(1)}, f32[2,72,7168]{2,1,0:T(8,128)}) fusion(bf16[2,72,7168]{2,1,0:T(8,128)(2,1)S(1)} %bitcast.23, f32[2,72,128]{2,1,0:T(8,128)S(1)} %factor6.1), kind=kOutput, calls=%fused_computation.17 | convolution fusion | flops 892846080 | bytes 8331264 | tf_op jit(solution)/shard_map/qsr,qri->qsi/dot_general | solution.py:773
  274.6 23.7 %stream7.1 = bf16[144,3584]{1,0:T(8,128)(2,1)S(1)} custom-call(bf16[144,7168]{1,0:T(8,128)(2,1)S(1)} %bitcast.25, bf16[7168,3584]{1,0:T(8,128)(2,1)} %w_ref.3), custom_call_target="tpu_custom_call" | custom-call | tf_op jit(solution)/shard_map/stream7/pallas_call | solution.py:470
  298.3 0.0 copy-start.1
  298.4 12.3 %convolution_convert_fusion.2 = bf16[2,72,2048]{2,1,0:T(8,128)(2,1)S(1)} fusion(bf16[2,72,3584]{2,1,0:T(8,128)(2,1)S(1)} %bitcast.24, bf16[2,3584,2048]{2,1,0:T(8,128)(2,1)} %get-tuple-element.13), kind=kOutput, calls=%fused_computation.2 | convolution fusion | flops 2114224128 | bytes 30982144 | tf_op jit(solution)/shard_map/qsj,qjp->qsp/dot_general | solution.py:779
  310.6 28.3 %sum8.1 = bf16[144,2048]{1,0:T(8,128)(2,1)S(1)} custom-call(bf16[144,2048]{1,0:T(8,128)(2,1)S(1)} %bitcast.26), custom_call_target="tpu_custom_call" | custom-call | tf_op jit(solution)/shard_map/sum8/pallas_call | solution.py:470
  338.9 0.0 copy-done.1
  338.9 1.5 convolution_convert_fusion.3.x_ref
  340.4 8.4 %sum9.1 = bf16[144,1024]{1,0:T(8,128)(2,1)S(1)} custom-call(bf16[144,1024]{1,0:T(8,128)(2,1)S(1)} %convolution_convert_fusion.3.x_ref), custom_call_target="tpu_custom_call" | custom-call | tf_op jit(solution)/shard_map/sum9/pallas_call | solution.py:470
  348.8 0.9 convert.1
  (2 shorter events, 0.0 us)
Async XLA Ops:
  0.6 71.3 %copy-start.2 = (bf16[72,1024]{1,0:T(8,128)(2,1)S(1)}, bf16[72,1024]{1,0:T(8,128)(2,1)}, u32[]{:S(2)}) copy-start(bf16[72,1024]{1,0:T(8,128)(2,1)} %param.11) | copy-start | bytes 442372
  142.3 1.8 copy-start
  298.3 40.5 %copy-start.1 = (bf16[1024,2048]{1,0:T(8,128)(2,1)S(1)}, bf16[1024,2048]{1,0:T(8,128)(2,1)}, u32[]{:S(2)}) copy-start(bf16[1024,2048]{1,0:T(8,128)(2,1)} %param.9) | copy-start | bytes 12582916

commit v3 on v2

--- a/solution.py
+++ b/solution.py
@@ -248,13 +248,13 @@
         for to in order[:-1]:
             second(to).wait_send()
 
-    return [begin, *[functools.partial(pair, to) for to in order[:-1]], total]
+    return [begin, *[functools.partial(pair, to) for to in order[:-1]], total], first, pair
 
 
 def col_sum_kernel(n, *refs):
     me = lax.axis_index("col")
     greet("col", n, me)
-    for stage in col_sum_stages(n, me, *refs):
+    for stage in col_sum_stages(n, me, *refs)[0]:
         stage()
 
 
@@ -378,6 +378,84 @@
     finish()
 
 
+def block_kernel(n, across, a_ref, w_ref, o_ref, w_buf, w_sem, part, *scratch):
+    me = lax.axis_index("col")
+    nz = n // 2
+    z, x = me // 2, lax.rem(me, 2)
+    width = o_ref.shape[1] // n
+
+    def block(i):
+        to = lax.rem(z + 1 + i // 2, nz)
+        return to * 2 + x + (1 - 2 * x) * (1 - lax.rem(i, 2))
+
+    def fetch(i):
+        at = pl.ds(pl.multiple_of(block(i) * width, width), width)
+        slot = lax.rem(i, DEPTH)
+        src = w_ref.at[:, :, at] if across else w_ref.at[at]
+        return pltpu.make_async_copy(src, w_buf.at[slot], w_sem.at[slot])
+
+    for i in range(DEPTH - 1):
+        fetch(i).start()
+    stages, first, pair = col_sum_stages(n, me, part, o_ref, *scratch)
+    greet("col", n, me)
+
+    def step(i, carry):
+        fetch(i).wait()
+
+        @pl.when(i + DEPTH - 1 < n)
+        def _():
+            fetch(i + DEPTH - 1).start()
+
+        slot = lax.rem(i, DEPTH)
+        if across:
+            pieces = [
+                jnp.dot(a_ref[q], w_buf[slot, q], preferred_element_type=F32)
+                for q in range(a_ref.shape[0])
+            ]
+            product = jnp.concatenate(pieces, axis=0)
+        else:
+            product = lax.dot_general(
+                a_ref[...], w_buf[slot], (((1,), (1,)), ((), ())), preferred_element_type=F32
+            )
+        part[:, pl.ds(pl.multiple_of(block(i) * width, width), width)] = product.astype(BF)
+
+        @pl.when(lax.rem(i, 2) == 0)
+        def _():
+            first(lax.rem(z + 1 + i // 2, nz)).start()
+
+        @pl.when((lax.rem(i, 2) == 1) & (i >= 3))
+        def _():
+            pair(lax.rem(z + i // 2, nz))
+
+        return carry
+
+    lax.fori_loop(0, n, step, 0)
+    stages[-1]()
+
+
+def dot_col_sum(a, w, across, n, number):
+    wide = w.shape[2] if across else w.shape[0]
+    rows = a.shape[0] * a.shape[1] if across else a.shape[0]
+    width = wide // n
+    if not (fits(rows, width, n) and n >= 2 * DEPTH and wide % n == 0 and a.shape[-1] % 128 == 0):
+        if across:
+            product = jnp.einsum("qsj,qjp->qsp", a, w, preferred_element_type=F32)
+        else:
+            product = dot(a, w, ((1,), (1,)))
+        return col_sum(product.astype(BF).reshape(rows, wide), n, number)
+    shape = (*w.shape[:2], width) if across else (width, w.shape[1])
+    scratch = [
+        pltpu.VMEM((DEPTH, *shape), BF),
+        pltpu.SemaphoreType.DMA((DEPTH,)),
+        pltpu.VMEM((rows, wide), BF),
+        *col_sum_scratch(n, rows, width),
+    ]
+    kernel = functools.partial(block_kernel, n, across)
+    return launch(
+        kernel, f"block{number}", number, (rows, wide), BF, scratch, a, w, specs=[VMEM, ANY]
+    )
+
+
 STREAM = 12
 
 
@@ -387,7 +465,7 @@
         n, me, a_ref, w_ref, o_ref, *scratch[:STREAM]
     )
     greet_both(ncol, n, mine, me)
-    begin, *pairs, total = col_sum_stages(ncol, mine, x_ref, s_ref, *scratch[STREAM:])
+    begin, *pairs, total = col_sum_stages(ncol, mine, x_ref, s_ref, *scratch[STREAM:])[0]
     begin()
     hooks = [(GAP * (k + 1), pair) for k, pair in enumerate(pairs)]
     late = [pair for at, pair in hooks if at >= count + LAG]
@@ -766,8 +844,7 @@
     scaled, reduced = scale_and_reduce(
         act_rot, grad_rot, eigen, sketch_rot, queries, (ncol, nrow), nrow, 2
     )
-    range_part = dot(reduced, basis_in, ((1,), (1,))).astype(BF)
-    range_rows = col_sum(range_part, ncol, 5).reshape(queries, size, -1)
+    range_rows = dot_col_sum(reduced, basis_in, False, ncol, 5).reshape(queries, size, -1)
     gram = jnp.einsum("qsi,qri->qsr", range_rows, range_rows, preferred_element_type=F32)
     inverse = inverse_factor(gram, nrow, 6)
     range_basis = jnp.einsum(
@@ -776,8 +853,7 @@
     basis_rows = range_basis.astype(BF).reshape(flat, -1)
     mapped = dot_row_sum(basis_rows, basis_in, nrow, 7)
     mapped = mapped.reshape(queries, size, -1)
-    core_part = jnp.einsum("qsj,qjp->qsp", mapped, scaled, preferred_element_type=F32)
-    core = col_sum(core_part.astype(BF).reshape(flat, -1), ncol, 8)
+    core = dot_col_sum(mapped, scaled, True, ncol, 8)
     projection_part = dot(core, basis_out, ((1,), (1,))).astype(BF)
     projected = row_sum(projection_part, nrow, 9)
     return range_basis, projected.astype(F32).reshape(queries, size, -1)

time: 350 us -> 321 us (0.917)
  matrix products: 45.2 us -> 10.4 us
  Pallas kernels: 299 us -> 305 us
    dot_general x3 -> x2, matrix products: 28.5 us -> 5.91 us  [dot(): lax.dot_general(a, b, (contract, ((), ())), preferred_element_type=F32)]
    dot_general x1 -> x0, matrix products: 12.3 us -> none  [on_device(): jnp.einsum('qsj,qjp->qsp', mapped, scaled, preferred_element_type=F32)]
    pallas_call x8, Pallas kernels: 299 us -> 305 us  [launch(): pl.pallas_call(kernel, name=name, out_shape=out if more is None else [out...]
where the time goes in v3:
time: 321 us
  Pallas kernels  305 us (95%)
  matrix products  10.4 us (3%)
  local copies, waits for them, and re-layouts  3.99 us (1%)
    pallas_call x8, Pallas kernels, launch(): pl.pallas_call(kernel, name=name, out_shape=out if more is None else [out...  305 us

profile of v3, /device:TPU:0, one launch (start us, length us, event | category | flops | bytes accessed | tf_op | source)
XLA Modules:
  0.0 320.6 jit_solution(16517523220465582113)
XLA Ops:
  0.6 0.0 copy-start.2
  0.6 1.0 copy.9
  1.6 1.2 copy.8
  2.9 69.0 %gather0.1 = (bf16[8,48,7168]{2,1,0:T(8,128)(2,1)}, bf16[4,96,1024]{2,1,0:T(8,128)(2,1)S(1)}) custom-call(bf16[48,7168]{1,0:T(8,128)(2,1)S(1)} %bitcast.21, bf16[96,1024]{1,0:T(8,128)(2,1)S(1)} %bitcast.23), custom_call_target="tpu_custom_call" | custom-call | tf_op jit(solution)/shard_map/gather0/pallas_call | solution.py:548
  71.9 0.0 copy-done.2
  71.9 4.4 %convolution_convert_fusion.x_ref = bf16[480,2048]{1,0:T(8,128)(2,1)S(1)} fusion(bf16[1024,2048]{1,0:T(8,128)(2,1)} %param.9, bf16[72,1024]{1,0:T(8,128)(2,1)S(1)} %copy-done.2, bf16[384,1024]{1,0:T(8,128)(2,1)S(1)} %bitcast.24), kind=kOutput, calls=%fused_computation | convolution fusion | flops 2017689600 | bytes 7094272 | tf_op jit(solution)/shard_map/dot_general | solution.py:824
  76.3 66.0 %stream1.1 = (bf16[384,3584]{1,0:T(8,128)(2,1)}, bf16[480,2048]{1,0:T(8,128)(2,1)S(1)}) custom-call(bf16[384,7168]{1,0:T(8,128)(2,1)} %bitcast.25, bf16[7168,3584]{1,0:T(8,128)(2,1)} %w_ref.5, bf16[480,2048]{1,0:T(8,128)(2,1)S(1)} %convolution_convert_fusion.x_ref), custom_call_target="tpu_custom_call" | custom-call | tf_op jit(solution)/shard_map/stream1/pallas_call | solution.py:548
  142.3 0.0 copy-start
  142.3 0.2 slice.9.grad_ref
  142.5 1.6 copy-done
  144.1 27.0 %scale2.1 = (bf16[2,3584,2048]{2,1,0:T(8,128)(2,1)}, bf16[144,3584]{1,0:T(8,128)(2,1)S(1)}) custom-call(bf16[384,3584]{1,0:T(8,128)(2,1)S(1)} %copy-done, bf16[384,2048]{1,0:T(8,128)(2,1)S(1)} %slice.9.grad_ref, bf16[72,2048]{1,0:T(8,128)(2,1)S(1)} %slice.10.sketch_ref, bf16[3584,2048]{1,0:T(8,128)(2,1)} %eigen_ref.1), custom_call_target="tpu_custom_call" | custom-call | tf_op jit(solution)/shard_map/scale2/pallas_call | solution.py:548
  171.1 61.0 %block5.1 = bf16[144,7168]{1,0:T(8,128)(2,1)S(1)} custom-call(bf16[144,3584]{1,0:T(8,128)(2,1)S(1)} %get-tuple-element.12.a_ref, bf16[7168,3584]{1,0:T(8,128)(2,1)} %w_ref.5), custom_call_target="tpu_custom_call" | custom-call | tf_op jit(solution)/shard_map/block5/pallas_call | solution.py:548
  232.1 0.7 fusion.15
  232.8 19.3 %factor6.1 = f32[2,72,128]{2,1,0:T(8,128)S(1)} custom-call(f32[2,72,128]{2,1,0:T(8,128)S(1)} %pad.9.g_ref), custom_call_target="tpu_custom_call" | custom-call | tf_op jit(solution)/shard_map/factor6/pallas_call | solution.py:548
  252.1 3.8 %fusion.14 = (bf16[2,72,7168]{2,1,0:T(8,128)(2,1)S(1)}, f32[2,72,7168]{2,1,0:T(8,128)}) fusion(bf16[2,72,7168]{2,1,0:T(8,128)(2,1)S(1)} %bitcast.18, f32[2,72,128]{2,1,0:T(8,128)S(1)} %factor6.1), kind=kOutput, calls=%fused_computation.15 | convolution fusion | flops 892846080 | bytes 8331264 | tf_op jit(solution)/shard_map/qsr,qri->qsi/dot_general | solution.py:850
  255.9 23.7 %stream7.1 = bf16[144,3584]{1,0:T(8,128)(2,1)S(1)} custom-call(bf16[144,7168]{1,0:T(8,128)(2,1)S(1)} %bitcast.19, bf16[7168,3584]{1,0:T(8,128)(2,1)} %w_ref.5), custom_call_target="tpu_custom_call" | custom-call | tf_op jit(solution)/shard_map/stream7/pallas_call | solution.py:548
  279.7 0.0 copy-start.1
  279.7 30.1 %block8.1 = bf16[144,2048]{1,0:T(8,128)(2,1)S(1)} custom-call(bf16[2,72,3584]{2,1,0:T(8,128)(2,1)S(1)} %bitcast.20, bf16[2,3584,2048]{2,1,0:T(8,128)(2,1)} %get-tuple-element.13.w_ref), custom_call_target="tpu_custom_call" | custom-call | tf_op jit(solution)/shard_map/block8/pallas_call | solution.py:548
  309.7 0.0 copy-done.1
  309.8 1.5 convolution_convert_fusion.1.x_ref
  311.3 8.4 %sum9.1 = bf16[144,1024]{1,0:T(8,128)(2,1)S(1)} custom-call(bf16[144,1024]{1,0:T(8,128)(2,1)S(1)} %convolution_convert_fusion.1.x_ref), custom_call_target="tpu_custom_call" | custom-call | tf_op jit(solution)/shard_map/sum9/pallas_call | solution.py:548
  319.7 0.9 convert.1
  (2 shorter events, 0.0 us)
Async XLA Ops:
  0.6 71.3 %copy-start.2 = (bf16[72,1024]{1,0:T(8,128)(2,1)S(1)}, bf16[72,1024]{1,0:T(8,128)(2,1)}, u32[]{:S(2)}) copy-start(bf16[72,1024]{1,0:T(8,128)(2,1)} %param.11) | copy-start | bytes 442372
  142.3 1.8 copy-start
  279.7 30.1 %copy-start.1 = (bf16[1024,2048]{1,0:T(8,128)(2,1)S(1)}, bf16[1024,2048]{1,0:T(8,128)(2,1)}, u32[]{:S(2)}) copy-start(bf16[1024,2048]{1,0:T(8,128)(2,1)} %param.9) | copy-start | bytes 12582916
